TPU v7x, 128 devices: a whole 4x4x4 slice. The times are simulated.
128 devices in a mesh: dp: 32 (over x, y, z_hi), pipe: 4 (over z_lo, core).
Axes of the slice: x: 4, y: 4, z: 4 (z_hi: 2, z_lo: 2; z = z_hi * 2 + z_lo), core: 2. Of those that a mesh axis runs over, the one named last changes fastest.
Arguments:
- master: float32 [4, 512, 8192], P('pipe', 'dp'), may hold values from -0.12 to 0.12
- moment1: float32 [4, 512, 8192], P('pipe', 'dp'), may hold values from -3 to 3
- moment2: float32 [4, 512, 8192], P('pipe', 'dp'), may hold values from 0.25 to 4.5
- quant_grad: bfloat16 [4, 512, 8192], P('pipe', 'dp'), may hold values from -120 to 120
- grad_exponent: int32 [4, 512], P('pipe', 'dp'), may hold values from -3 to 2
- replica_params: bfloat16 [4, 32, 512, 8192], P('pipe', 'dp'), as said below
- failed: int32 [4, 2], replicated, may hold values from 0 to 31, as said below
- dest: int32 [4, 512], replicated, may hold values from 0 to 511, as said below
Outputs:
- new_master: float32 [4, 512, 8192], P('pipe', 'dp')
- new_moment1: float32 [4, 512, 8192], P('pipe', 'dp')
- new_moment2: float32 [4, 512, 8192], P('pipe', 'dp')
Inputs may be any that keep to these rules, and one draw needn't show every extreme that they name: `failed`: each group lists 2 distinct ranks; group 0 lists ranks 1 and 16; in every other group some rows of the first listed rank have new positions among the rows of the second listed rank (new position // 16). `dest`: each group's row is a permutation of its rows; the 16 rows of one rank (old rows r * 16 to r * 16 + 15) land in at most 1 row of any one rank's new rows (new position // 16), and some pair of ranks reaches 1 in every group. `replica_params`: within a group the copies of ranks not listed in failed are equal; the copies of listed ranks are zero.
All inputs are finite; a program needn't handle non-finite values.
Results may differ from a plain program's by a relative error of at most 0.0003.
Values may be sent and summed in bfloat16 or wider, within the bound.
A program may use at most 64 MiB of HBM per device.

v0:
```python
import jax
import jax.numpy as jnp
from jax import lax
from jax.sharding import PartitionSpec as P

STEP = 20


beta_one = 0.9
beta_two = 0.95
learn_rate = 0.00015
decay_rate = 0.1
adam_eps = 1e-08
clip_eps = 1e-06


def from_root(value, axis, source):
    kept = jnp.where(lax.axis_index(axis) == source, value, 0).astype(value.dtype)
    return lax.psum(kept, axis)


def adam_step(weights, first, second, grads):
    first_new = beta_one * first + (1.0 - beta_one) * grads
    second_new = beta_two * second + (1.0 - beta_two) * grads * grads
    corr_one = 1.0 - beta_one**STEP
    corr_two = 1.0 - beta_two**STEP
    direction = (
        first_new / corr_one / (jnp.sqrt(second_new / corr_two) + adam_eps) + decay_rate * weights
    )
    return (weights - learn_rate * direction, first_new, second_new)


def local(master, moment1, moment2, quant_grad, grad_exponent, replica_params, failed, dest):
    group_idx = lax.axis_index("pipe")
    my_rank = lax.axis_index("dp")
    ranks_count = lax.axis_size("dp")
    shard_rows = master.shape[1]
    row_width = master.shape[2]
    fail_count = failed.shape[1]
    peer_slots = (shard_rows + ranks_count - 1) // ranks_count
    fail_row = lax.dynamic_index_in_dim(failed, group_idx, 0, keepdims=False)
    dest_row = lax.dynamic_index_in_dim(dest, group_idx, 0, keepdims=False)
    rank_ids = jnp.arange(ranks_count, dtype=jnp.int32)
    is_alive = jnp.all(rank_ids[:, None] != fail_row[None, :], axis=1)
    own_fail = fail_row == my_rank
    is_lost = jnp.any(own_fail)
    copy_rows = replica_params[0, 0]
    first_root = jnp.min(jnp.where(is_alive, rank_ids, ranks_count))
    bf_zero = jnp.zeros((), jnp.bfloat16)
    local_ids = jnp.arange(shard_rows, dtype=jnp.int32)
    group_ids = jnp.arange(dest_row.shape[0], dtype=jnp.int32)
    targets = (dest_row // shard_rows).reshape(ranks_count, shard_rows)
    earlier = local_ids[None, :] < local_ids[:, None]
    same_target = targets[:, :, None] == targets[:, None, :]
    order_in = jnp.sum((same_target & earlier[None, :, :]).astype(jnp.int32), axis=2)
    my_targets = lax.dynamic_index_in_dim(targets, my_rank, 0, keepdims=False)
    my_order = lax.dynamic_index_in_dim(order_in, my_rank, 0, keepdims=False)
    slot_ids = jnp.arange(peer_slots, dtype=jnp.int32)
    pick_mask = (my_targets[None, None, :] == rank_ids[:, None, None]) & (
        my_order[None, None, :] == slot_ids[None, :, None]
    )
    send_index = jnp.sum(jnp.where(pick_mask, local_ids[None, None, :], 0), axis=2).reshape(-1)
    new_rows = my_rank * shard_rows + local_ids
    match_mask = dest_row[None, :] == new_rows[:, None]
    source_row = jnp.sum(jnp.where(match_mask, group_ids[None, :], 0), axis=1)
    source_rank = source_row // shard_rows
    source_order = order_in.reshape(-1)[source_row]
    recv_index = source_rank * peer_slots + source_order
    master_extra = None
    lost_blocks = jnp.stack(
        [
            lax.dynamic_slice_in_dim(copy_rows, fail_row[piece_idx] * shard_rows, shard_rows, 0)
            for piece_idx in range(fail_count)
        ]
    )
    lost_blocks = jnp.where(my_rank == first_root, lost_blocks, bf_zero)
    received_rows = from_root(lost_blocks, "dp", first_root)
    recovered = jnp.sum(
        jnp.where(own_fail[:, None, None], received_rows.astype(jnp.float32), jnp.float32(0.0)),
        axis=0,
    )
    start_master = jnp.where(is_lost, recovered, master[0])
    start_first = jnp.where(is_lost, jnp.float32(0.0), moment1[0])
    start_second = jnp.where(is_lost, jnp.float32(0.0), moment2[0])
    grad = (
        quant_grad[0].astype(jnp.float32) * jnp.exp2(grad_exponent[0].astype(jnp.float32))[:, None]
    )
    grad_total = lax.psum(jnp.sum(grad * grad), ("dp", "pipe"))
    elem_count = lax.axis_size("dp") * lax.axis_size("pipe") * shard_rows * row_width
    clip_scale = jnp.minimum(1.0, 1.0 / jnp.sqrt(grad_total / elem_count + clip_eps))
    clipped = grad * clip_scale

    def to_buffer(values):
        return values[send_index].reshape(ranks_count, peer_slots, row_width)

    w_next, m_next, v_next = adam_step(start_master, start_first, start_second, clipped)
    received = (
        lax.all_to_all(to_buffer(w_next), "dp", split_axis=0, concat_axis=0, tiled=True),
        lax.all_to_all(to_buffer(m_next), "dp", split_axis=0, concat_axis=0, tiled=True),
        lax.all_to_all(to_buffer(v_next), "dp", split_axis=0, concat_axis=0, tiled=True),
    )
    placed = tuple(
        (values.reshape(ranks_count * peer_slots, row_width)[recv_index] for values in received)
    )
    placed_master = placed[0]
    return (placed_master[None], placed[1][None], placed[2][None])


def solution(mesh):
    in_specs = (
        P("pipe", "dp", None),
        P("pipe", "dp", None),
        P("pipe", "dp", None),
        P("pipe", "dp", None),
        P("pipe", "dp"),
        P("pipe", "dp", None, None),
        P(),
        P(),
    )
    out_specs = (P("pipe", "dp", None), P("pipe", "dp", None), P("pipe", "dp", None))
    return jax.shard_map(local, mesh=mesh, in_specs=in_specs, out_specs=out_specs, check_vma=False)
```

profile of v0, /device:TPU:0, one launch (start us, length us, event | category | flops | bytes accessed | tf_op | source)
XLA Modules:
  0.0 445.7 jit_solution(17643683241588214400)
XLA Ops:
  7.2 0.0 all-reduce.2.cloned.1.call-start
  7.2 0.9 fusion.19
  8.1 0.5 fusion.20
  9.9 0.1 compare_reduce_fusion
  10.0 0.6 select_reduce_fusion.3
  11.3 1.1 dynamic-slice_bitcast_fusion.1
  12.4 0.9 fusion.1
  13.2 0.0 all-reduce.2.cloned.1.call-update
  13.3 0.7 exponential_bitcast_fusion
  13.9 1.8 fusion.6
  15.7 69.2 %psum.15 = f32[]{:T(128)} all-reduce(f32[]{:T(128)} %fusion.6), channel_id=1, replica_groups=mesh['dp'=32,'pipe'=4] {'dp','pipe'}, use_global_device_ids=true, to_apply=%region_6.7 | all-reduce | flops 1 | bytes 8 | tf_op jit(solution)/shard_map/psum | solution.py:88
  85.6 0.5 broadcast.320
  86.1 1.4 fusion.15
  87.4 0.1 squeeze.23
  87.5 0.1 copy.20
  87.6 0.1 convert_reduce_fusion
  87.7 0.2 fusion.10
  87.9 0.1 select_reduce_fusion.2
  88.0 0.6 fusion.18
  88.7 277.0 %all-reduce.2.cloned.1.call-done = bf16[2,16,8192]{2,1,0:T(8,128)(2,1)} async-done(((bf16[2,16,8192]{2,1,0:T(8,128)(2,1)}), bf16[2,16,8192]{2,1,0:T(8,128)(2,1)}) %all-reduce.2.cloned.1.call-update) | async-done | bytes 524304 | tf_op jit(solution)/shard_map/psum | solution.py:19
  365.7 1.3 select_reduce_fusion
  367.0 2.7 multiply_subtract_fusion
  369.7 0.9 gather_fusion
  370.6 2.1 copy.22
  372.7 10.0 %all-to-all-start = ((f32[32,1,8192]{2,1,0:T(1,128)}), f32[32,1,8192]{2,1,0:T(1,128)S(1)}, u32[]{:S(2)}, u32[]{:S(2)}) async-start(f32[32,1,8192]{2,1,0:T(1,128)} %copy.22), calls=%async_computation | async-start | bytes 2097152 | tf_op jit(solution)/shard_map/all_to_all | solution.py:98
  382.7 0.9 gather_fusion.3
  383.6 2.1 copy.24
  385.7 12.2 %all-to-all-done = f32[32,1,8192]{2,1,0:T(1,128)S(1)} async-done(((f32[32,1,8192]{2,1,0:T(1,128)}), f32[32,1,8192]{2,1,0:T(1,128)S(1)}, u32[]{:S(2)}, u32[]{:S(2)}) %all-to-all-start) | async-done | bytes 1048608 | tf_op jit(solution)/shard_map/all_to_all | solution.py:98
  397.8 4.7 %all-to-all-start.1 = ((f32[32,1,8192]{2,1,0:T(1,128)}), f32[32,1,8192]{2,1,0:T(1,128)}, u32[]{:S(2)}, u32[]{:S(2)}) async-start(f32[32,1,8192]{2,1,0:T(1,128)} %copy.24), calls=%async_computation.1 | async-start | bytes 2097152 | tf_op jit(solution)/shard_map/all_to_all | solution.py:99
  402.5 0.9 gather_fusion.5
  403.4 2.1 copy.25
  405.5 12.5 %all-to-all-done.1 = f32[32,1,8192]{2,1,0:T(1,128)} async-done(((f32[32,1,8192]{2,1,0:T(1,128)}), f32[32,1,8192]{2,1,0:T(1,128)}, u32[]{:S(2)}, u32[]{:S(2)}) %all-to-all-start.1) | async-done | bytes 1048608 | tf_op jit(solution)/shard_map/all_to_all | solution.py:99
  418.0 3.9 all-to-all-start.2
  421.9 0.1 copy.23
  422.0 0.1 reshape.317
  422.1 0.2 select_reduce_fusion.1
  422.3 0.7 gather_fusion.1
  423.0 0.6 copy.34
  423.6 1.5 gather_fusion.2
  425.1 1.8 copy.33
  426.9 1.5 gather_fusion.4
  428.4 8.3 %all-to-all-done.2 = f32[32,1,8192]{2,1,0:T(1,128)S(1)} async-done(((f32[32,1,8192]{2,1,0:T(1,128)}), f32[32,1,8192]{2,1,0:T(1,128)S(1)}, u32[]{:S(2)}, u32[]{:S(2)}) %all-to-all-start.2) | async-done | bytes 1048608 | tf_op jit(solution)/shard_map/all_to_all | solution.py:100
  436.7 0.6 copy.32
  437.3 1.5 gather_fusion.6
  (10 shorter events, 0.1 us)
Async XLA Ops:
  7.2 358.5 %all-reduce.2.cloned.1.call-start = ((), (), s32[]{:S(2)}) async-start(), calls=%async_computation.3 | async-start | bytes 1048576 | tf_op jit(solution)/shard_map/psum | solution.py:19
  372.7 25.1 %all-to-all-start = ((f32[32,1,8192]{2,1,0:T(1,128)}), f32[32,1,8192]{2,1,0:T(1,128)S(1)}, u32[]{:S(2)}, u32[]{:S(2)}) async-start(f32[32,1,8192]{2,1,0:T(1,128)} %copy.22), calls=%async_computation | async-start | bytes 2097152 | tf_op jit(solution)/shard_map/all_to_all | solution.py:98
  397.8 20.2 %all-to-all-start.1 = ((f32[32,1,8192]{2,1,0:T(1,128)}), f32[32,1,8192]{2,1,0:T(1,128)}, u32[]{:S(2)}, u32[]{:S(2)}) async-start(f32[32,1,8192]{2,1,0:T(1,128)} %copy.24), calls=%async_computation.1 | async-start | bytes 2097152 | tf_op jit(solution)/shard_map/all_to_all | solution.py:99
  418.0 18.7 %all-to-all-start.2 = ((f32[32,1,8192]{2,1,0:T(1,128)}), f32[32,1,8192]{2,1,0:T(1,128)S(1)}, u32[]{:S(2)}, u32[]{:S(2)}) async-start(f32[32,1,8192]{2,1,0:T(1,128)} %copy.25), calls=%async_computation.2 | async-start | bytes 2097152 | tf_op jit(solution)/shard_map/all_to_all | solution.py:100
Sparse Core Ops, SparseCore 0:
  13.4 352.2 all-reduce.1
where the time goes:
time: 446 us
  waiting for transfers between devices  310 us (70%)
  blocking collectives  69.2 us (16%)
  local copies, waits for them, and re-layouts  21.8 us (5%)
  starting transfers between devices  18.6 us (4%)
  between operations  16.8 us (4%)
  other arithmetic  9.3 us (2%)
    psum x1, waiting for transfers between devices, from_root(): return lax.psum(kept, axis)  277 us
    psum x1, blocking collectives, local(): grad_total = lax.psum(jnp.sum(grad * grad), ('dp', 'pipe'))  69.2 us
    all_to_all x1, waiting for transfers between devices, local(): lax.all_to_all(to_buffer(m_next), 'dp', split_axis=0, concat_axis=0, tile...  12.5 us
    all_to_all x1, waiting for transfers between devices, local(): lax.all_to_all(to_buffer(w_next), 'dp', split_axis=0, concat_axis=0, tile...  12.2 us
    all_to_all x1, starting transfers between devices, local(): lax.all_to_all(to_buffer(w_next), 'dp', split_axis=0, concat_axis=0, tile...  9.98 us
  transfers between devices with their start and end apart: 4, of which 4 were waited for; matrix products, arithmetic and copies ran while one was open for 4% of the time, Pallas kernels for 0%

commit v1 on v0

v1 whole, which is shorter than its diff:
```python
import functools
import math

import jax
import jax.numpy as jnp
from jax import lax
from jax.experimental import pallas as pl
from jax.experimental.pallas import tpu as pltpu
from jax.sharding import PartitionSpec as P

STEP = 20

beta_one = 0.9
beta_two = 0.95
learn_rate = 0.00015
decay_rate = 0.1
adam_eps = 1e-08
clip_eps = 1e-06

corr_one = 1.0 - beta_one**STEP
corr_two = 1.0 - beta_two**STEP

MESH = pl.DeviceIdType.MESH
DP = 32
PIPE = 4
K = 16
D = 8192
HALF = D // 2
LANES = 128
W_COLS = HALF + 3 * LANES
CHUNKS = 4
CW = D // CHUNKS
STEP_COLS = 1024
TILES = STEP_COLS // LANES

SCALE_UNIT = 65536.0
TINY = 1e-30
LOG_LOW = -2.2
LOG_SPAN = 16.0
LOG_UNIT = 65535.0 / LOG_SPAN


def cols(step, width=STEP_COLS, base=0):
    return pl.ds(pl.multiple_of(base + step * width, LANES), width)


def tiled(scale):
    return jnp.concatenate([scale] * TILES, axis=1)


def fold(acc, op):
    out = acc[:, :LANES]
    for t in range(1, TILES):
        out = op(out, acc[:, t * LANES : (t + 1) * LANES])
    return out


def scale_code(scale):
    return jnp.ceil(jnp.log2(jnp.maximum(scale, TINY)) * SCALE_UNIT).astype(jnp.int32)


def scale_value(code):
    return jnp.exp2(code.astype(jnp.float32) * (1.0 / SCALE_UNIT))


def nearest(x):
    return jnp.floor(x + 0.5).astype(jnp.int32)


def peer(me, code):
    x = lax.rem(me // 8 + code // 8, 4)
    y = lax.rem((me // 2) % 4 + (code // 2) % 4, 4)
    z = lax.rem(me % 2 + code % 2, 2)
    return x * 8 + y * 2 + z


def offset(me, source):
    x = lax.rem(me // 8 - source // 8 + 4, 4)
    y = lax.rem((me // 2) % 4 - (source // 2) % 4 + 4, 4)
    z = lax.rem(me % 2 - source % 2 + 2, 2)
    return x * 8 + y * 2 + z


def order(k):
    return lax.rem(k * 11, DP)


def kernel(
    master_ref, moment1_ref, moment2_ref, quant_ref, expo_ref, replica_ref, failed_ref, dest_ref,
    w_ref, m_ref, u_ref,
    master, moment1, moment2, quant, expo, replica, dest_v, failed_s, dest_s,
    part, parts, w_code, w_send, w_recv, w_rows, mv_code, mv_send, mv_recvs, mv_rows,
    scales, rows_s, slots_s, in_sem, part_ssem, part_rsem, w_ssem, w_rsem, mv_ssem, mv_rsem,
):
    me = lax.axis_index("dp")
    group = lax.axis_index("pipe")

    loads = [
        pltpu.make_async_copy(src, dst, in_sem.at[i])
        for i, (src, dst) in enumerate(
            (
                (quant_ref, quant),
                (expo_ref, expo),
                (dest_ref, dest_v),
                (dest_ref, dest_s),
                (failed_ref, failed_s),
                (master_ref, master),
                (moment1_ref, moment1),
                (replica_ref, replica),
                (moment2_ref, moment2),
            )
        )
    ]
    barrier = pltpu.get_barrier_semaphore()

    def greet(c, carry):
        pl.semaphore_signal(
            barrier,
            inc=1,
            device_id=(lax.rem(me + c // PIPE, DP), lax.rem(group + c % PIPE, PIPE)),
            device_id_type=MESH,
        )
        return carry

    loads[0].start()
    loads[1].start()
    lax.fori_loop(1, DP * PIPE, greet, 0)
    for load in loads[2:]:
        load.start()

    loads[0].wait()
    loads[1].wait()
    line = lax.broadcasted_iota(jnp.int32, (K, K), 0)
    place = lax.broadcasted_iota(jnp.int32, (K, K), 1)
    expo_rows = jnp.sum(
        jnp.where(line == place, jnp.broadcast_to(expo[...].astype(jnp.float32), (K, K)), 0.0),
        axis=1,
        keepdims=True,
    )
    grad_scale = jnp.exp2(expo_rows)

    def scan_grad(step, carry):
        total, largest = carry
        x = quant[:, cols(step)].astype(jnp.float32)
        return total + x * x, jnp.maximum(largest, jnp.abs(x))

    zero_step = jnp.zeros((K, STEP_COLS), jnp.float32)
    total, largest = lax.fori_loop(0, D // STEP_COLS, scan_grad, (zero_step, zero_step))
    squares = fold(total, jnp.add) * (grad_scale * grad_scale)
    part[0:1, :] = jnp.sum(squares, axis=0, keepdims=True)
    grad_most = fold(largest, jnp.maximum) * ((1.0 - beta_one) * grad_scale)

    for load in loads[2:5]:
        load.wait()
    fail_a = failed_s[group, 0]
    fail_b = failed_s[group, 1]
    me_failed = (me == fail_a) | (me == fail_b)

    def find_slot(code, carry):
        target = peer(me, code)
        found = jnp.int32(0)
        for i in range(K):
            found = jnp.where((dest_s[group, me * K + i] >> 4) == target, i + 1, found)
        slots_s[code] = found
        return carry

    lax.fori_loop(0, DP, find_slot, 0)

    def row_for(code):
        found = slots_s[code]
        return jnp.maximum(found - 1, 0), found > 0

    dest_row = dest_v[pl.ds(group, 1), :]
    old_row = lax.broadcasted_iota(jnp.int32, (1, DP * K), 1)
    old_rank = old_row >> 4
    new_rank = dest_row >> 4
    rank_bit = lax.broadcasted_iota(jnp.int32, (1, DP), 1)
    alive_bits = jnp.sum(
        jnp.where((rank_bit == fail_a) | (rank_bit == fail_b), 0, 1 << rank_bit)
    )

    def helper_bits(receiver):
        bits = jnp.sum(jnp.where(new_rank == receiver, 1 << old_rank, 0))
        return alive_bits & ~bits

    def helper_row(receiver):
        bits = helper_bits(receiver)
        first = jnp.max(
            jnp.where((new_rank == receiver) & (old_rank == fail_a), old_row & 15, 0)
        )
        second = jnp.max(
            jnp.where((new_rank == receiver) & (old_rank == fail_b), old_row & 15, 0)
        )
        able = ((bits >> me) & 1) == 1
        lower = bits & ((1 << me) - 1)
        is_first = able & (lower == 0)
        is_second = able & (lower != 0) & ((lower & (lower - 1)) == 0)
        return jnp.where(is_first, K + first, jnp.where(is_second, 2 * K + second, 0))

    help_a = helper_row(fail_a)
    help_b = helper_row(fail_b)

    pl.semaphore_wait(barrier, DP * PIPE - 1)

    def part_copy(c):
        return pltpu.make_async_remote_copy(
            src_ref=part.at[pl.ds(0, 1)],
            dst_ref=parts.at[pl.ds(c, 1)],
            send_sem=part_ssem.at[c],
            recv_sem=part_rsem.at[c],
            device_id=(lax.rem(me + c // PIPE, DP), lax.rem(group + c % PIPE, PIPE)),
            device_id_type=MESH,
        )

    def send_part(c, carry):
        part_copy(c).start()
        return carry

    lax.fori_loop(1, DP * PIPE, send_part, 0)

    loads[5].wait()
    loads[6].wait()
    loads[7].wait()

    def weights(kind, step, base=0):
        if kind == 0:
            return master[:, cols(step, base=base)]
        rank = fail_a if kind == 1 else fail_b
        return replica[rank, :, cols(step, base=base)].astype(jnp.float32)

    def scan_moment(step, largest):
        return jnp.maximum(largest, jnp.abs(moment1[:, cols(step)]))

    keep = jnp.where(me_failed, 0.0, 1.0).astype(jnp.float32)
    largest = lax.fori_loop(0, D // STEP_COLS, scan_moment, zero_step)
    moment_code = scale_code(fold(largest, jnp.maximum) * (keep * beta_one))
    grad_code = scale_code(grad_most)
    scales[0:K, :] = scale_value(moment_code)
    scales[K : 2 * K, :] = scale_value(grad_code)

    for kind in range(3):
        rows = pl.ds(kind * K, K)

        def scan_weights(step, largest, kind=kind):
            return jnp.maximum(largest, jnp.abs(weights(kind, step)))

        largest = lax.fori_loop(0, D // STEP_COLS, scan_weights, zero_step)
        code = scale_code(fold(largest, jnp.maximum))
        to_code = tiled(32767.0 / scale_value(code))
        w_code[rows, HALF : HALF + LANES] = code
        w_code[rows, HALF + LANES : HALF + 2 * LANES] = moment_code
        w_code[rows, HALF + 2 * LANES : HALF + 3 * LANES] = grad_code

        def code_weights(step, carry, kind=kind, rows=rows, to_code=to_code):
            low = nearest(weights(kind, step) * to_code)
            high = nearest(weights(kind, step, HALF) * to_code)
            w_code[rows, cols(step)] = (high << 16) | (low & 0xFFFF)
            return carry

        lax.fori_loop(0, HALF // STEP_COLS, code_weights, 0)

    def w_copy(k):
        code = order(k)
        return pltpu.make_async_remote_copy(
            src_ref=w_send.at[pl.ds(code, 1)],
            dst_ref=w_recv.at[pl.ds(code, 1)],
            send_sem=w_ssem.at[code],
            recv_sem=w_rsem.at[code],
            device_id=(peer(me, code), group),
            device_id_type=MESH,
        )

    def w_slot(k):
        code = order(k)
        target = peer(me, code)
        row, has = row_for(code)
        helped = jnp.where(target == fail_a, help_a, jnp.where(target == fail_b, help_b, 0))
        w_send[pl.ds(code, 1), :] = w_code[pl.ds(jnp.where(has, row, helped), 1), :]

    def send_w(k, carry):
        w_slot(k)
        w_copy(k - 1).start()
        return carry

    w_slot(1)
    lax.fori_loop(2, DP, send_w, 0)
    w_copy(DP - 1).start()
    own_row, _ = row_for(0)
    w_recv[0:1, :] = w_code[pl.ds(own_row, 1), :]

    def find_row(j, taken):
        row = jnp.max(jnp.where(dest_row == me * K + j, old_row, 0))
        rows_s[j] = row
        return taken

    lax.fori_loop(0, K, find_row, 0)
    bits = helper_bits(me)
    lane = lax.broadcasted_iota(jnp.int32, (1, LANES), 1)
    able = (lane < DP) & (((bits >> (lane & 31)) & 1) == 1)
    helper_one = jnp.min(jnp.where(able, lane, DP - 1))
    helper_two = jnp.min(jnp.where(able & (lane > helper_one), lane, DP - 1))

    def wait_part(c, carry):
        part_copy(c).wait_recv()
        return carry

    lax.fori_loop(1, DP * PIPE, wait_part, 0)
    loads[8].wait()
    parts[0:1, :] = part[0:1, :]
    grad_total = jnp.sum(
        jnp.sum(parts[...], axis=0, keepdims=True), axis=1, keepdims=True
    )
    clip = jnp.minimum(1.0, lax.rsqrt(grad_total / float(DP * PIPE * K * D) + clip_eps))

    bound = scales[0:K, :] + clip * scales[K : 2 * K, :]
    to_unit = tiled(1.0 / bound)
    clip_scale = grad_scale * clip

    def mv_copy(chunk, k):
        code = order(k)
        return pltpu.make_async_remote_copy(
            src_ref=mv_send.at[chunk, pl.ds(code, 1)],
            dst_ref=mv_recvs[chunk].at[pl.ds(code, 1)],
            send_sem=mv_ssem.at[chunk, code],
            recv_sem=mv_rsem.at[chunk, code],
            device_id=(peer(me, code), group),
            device_id_type=MESH,
        )

    def mv_slot(chunk, k):
        code = order(k)
        row, _ = row_for(code)
        mv_send[chunk, pl.ds(code, 1), :] = mv_code[chunk, pl.ds(row, 1), :]

    def send_chunk(chunk):
        def code_moments(step, carry):
            here = cols(chunk * (CW // STEP_COLS) + step)
            clipped = quant[:, here].astype(jnp.float32) * clip_scale
            first = (keep * beta_one) * moment1[:, here] + (1.0 - beta_one) * clipped
            second = (keep * beta_two) * moment2[:, here] + (1.0 - beta_two) * clipped * clipped
            root = jnp.sqrt(jnp.abs(first) * to_unit) * 32767.0
            high = nearest(jnp.where(first < 0.0, -root, root))
            level = (jnp.log2(jnp.maximum(second, 0.2)) - LOG_LOW) * LOG_UNIT
            low = nearest(jnp.clip(level, 0.0, 65535.0))
            mv_code[chunk, :, cols(step)] = (high << 16) | low
            return carry

        lax.fori_loop(0, CW // STEP_COLS, code_moments, 0)

        def send_mv(k, carry):
            mv_slot(chunk, k)
            mv_copy(chunk, k - 1).start()
            return carry

        mv_slot(chunk, 1)
        lax.fori_loop(2, DP, send_mv, 0)
        mv_copy(chunk, DP - 1).start()
        mv_recvs[chunk][0:1, :] = mv_code[chunk, pl.ds(own_row, 1), :]

    for chunk in range(CHUNKS):
        send_chunk(chunk)

    def wait_w(k, carry):
        w_copy(k).wait_recv()
        return carry

    lax.fori_loop(1, DP, wait_w, 0)

    def place_w(j, carry):
        row = rows_s[j]
        source = row >> 4
        in_second = source == fail_b
        lost = (source == fail_a) | in_second
        helper = jnp.where(in_second, helper_two, helper_one)
        sender = jnp.where(lost & me_failed, helper, source)
        from_peer = w_recv[pl.ds(offset(me, sender), 1), :]
        block = jnp.where(in_second, 2 * K, K)
        local = w_code[pl.ds(jnp.where(lost, block + (row & 15), 0), 1), :]
        lost_here = lost & jnp.logical_not(me_failed)
        w_rows[pl.ds(j, 1), 0:HALF + LANES] = jnp.where(
            lost_here, local[:, 0:HALF + LANES], from_peer[:, 0:HALF + LANES]
        )
        owner = w_recv[pl.ds(offset(me, source), 1), HALF + LANES : W_COLS]
        w_rows[pl.ds(j, 1), HALF + LANES : W_COLS] = owner
        parts[pl.ds(j, 1), :] = jnp.broadcast_to(jnp.where(lost, 1.0, 0.0), (1, LANES))
        return carry

    lax.fori_loop(0, K, place_w, 0)
    w_unit = tiled(scale_value(w_rows[:, HALF : HALF + LANES]) * (1.0 / 32767.0))

    def decode_w(step, carry):
        word = w_rows[:, cols(step)]
        w_ref[:, cols(step)] = ((word << 16) >> 16).astype(jnp.float32) * w_unit
        w_ref[:, cols(step, base=HALF)] = (word >> 16).astype(jnp.float32) * w_unit
        return carry

    lax.fori_loop(0, HALF // STEP_COLS, decode_w, 0)
    came_bound = scale_value(w_rows[:, HALF + LANES : HALF + 2 * LANES]) + clip * scale_value(
        w_rows[:, HALF + 2 * LANES : W_COLS]
    )
    from_unit = tiled(came_bound * (1.0 / (32767.0 * 32767.0)))
    row_lost = tiled(parts[0:K, :]) > 0.5

    def take_chunk(chunk):
        def wait_mv(k, carry):
            mv_copy(chunk, k).wait_recv()
            return carry

        lax.fori_loop(1, DP, wait_mv, 0)

        def place_mv(j, carry):
            source = rows_s[j] >> 4
            mv_rows[chunk, pl.ds(j, 1), :] = mv_recvs[chunk][
                pl.ds(offset(me, source), 1), :
            ]
            return carry

        lax.fori_loop(0, K, place_mv, 0)

        def decode_mv(step, carry):
            here = cols(chunk * (CW // STEP_COLS) + step)
            word = mv_rows[chunk, :, cols(step)]
            high = (word >> 16).astype(jnp.float32)
            low = (word & 0xFFFF).astype(jnp.float32)
            first = high * jnp.abs(high) * from_unit
            grown = jnp.exp2(low * (0.5 / LOG_UNIT) + 0.5 * (LOG_LOW - math.log2(corr_two)))
            m_ref[:, here] = first
            u_ref[:, here] = jnp.where(
                row_lost, jnp.abs(first) * math.sqrt(5.0 / corr_two), grown
            )
            return carry

        lax.fori_loop(0, CW // STEP_COLS, decode_mv, 0)

    for chunk in range(CHUNKS):
        take_chunk(chunk)

    def left_part(c, carry):
        part_copy(c).wait_send()
        return carry

    def left_w(k, carry):
        w_copy(k).wait_send()
        for chunk in range(CHUNKS):
            mv_copy(chunk, k).wait_send()
        return carry

    lax.fori_loop(1, DP * PIPE, left_part, 0)
    lax.fori_loop(1, DP, left_w, 0)


def local(master, moment1, moment2, quant_grad, grad_exponent, replica_params, failed, dest):
    f32, i32 = jnp.float32, jnp.int32
    hbm = pl.BlockSpec(memory_space=pl.ANY)
    vmem = pl.BlockSpec(memory_space=pltpu.VMEM)
    dma = pltpu.SemaphoreType.DMA
    start, first, root = pl.pallas_call(
        kernel,
        out_shape=(jax.ShapeDtypeStruct((K, D), f32),) * 3,
        in_specs=[hbm] * 8,
        out_specs=(vmem,) * 3,
        scratch_shapes=[
            pltpu.VMEM((K, D), f32),
            pltpu.VMEM((K, D), f32),
            pltpu.VMEM((K, D), f32),
            pltpu.VMEM((K, D), jnp.bfloat16),
            pltpu.VMEM((1, K), i32),
            pltpu.VMEM((DP, K, D), jnp.bfloat16),
            pltpu.VMEM((PIPE, DP * K), i32),
            pltpu.SMEM((PIPE, 2), i32),
            pltpu.SMEM((PIPE, DP * K), i32),
            pltpu.VMEM((8, LANES), f32),
            pltpu.VMEM((DP * PIPE, LANES), f32),
            pltpu.VMEM((3 * K, W_COLS), i32),
            pltpu.VMEM((DP, W_COLS), i32),
            pltpu.VMEM((DP, W_COLS), i32),
            pltpu.VMEM((K, W_COLS), i32),
            pltpu.VMEM((CHUNKS, K, CW), i32),
            pltpu.VMEM((CHUNKS, DP, CW), i32),
            [pltpu.VMEM((DP, CW), i32)] * CHUNKS,
            pltpu.VMEM((CHUNKS, K, CW), i32),
            pltpu.VMEM((2 * K, LANES), f32),
            pltpu.SMEM((K,), i32),
            pltpu.SMEM((DP,), i32),
            dma((9,)),
            dma((DP * PIPE,)),
            dma((DP * PIPE,)),
            dma((DP,)),
            dma((DP,)),
            dma((CHUNKS, DP)),
            dma((CHUNKS, DP)),
        ],
        compiler_params=pltpu.CompilerParams(
            collective_id=0, has_side_effects=True, vmem_limit_bytes=56 * 2**20
        ),
        name="recover_step",
    )(
        master[0],
        moment1[0],
        moment2[0],
        quant_grad[0],
        grad_exponent,
        replica_params[0, 0].reshape(DP, K, D),
        failed,
        dest,
    )
    direction = first / corr_one / (root + adam_eps) + decay_rate * start
    return (
        (start - learn_rate * direction)[None],
        first[None],
        (corr_two * root * root)[None],
    )


def solution(mesh):
    in_specs = (
        P("pipe", "dp", None),
        P("pipe", "dp", None),
        P("pipe", "dp", None),
        P("pipe", "dp", None),
        P("pipe", "dp"),
        P("pipe", "dp", None, None),
        P(),
        P(),
    )
    out_specs = (P("pipe", "dp", None), P("pipe", "dp", None), P("pipe", "dp", None))
    return jax.shard_map(local, mesh=mesh, in_specs=in_specs, out_specs=out_specs, check_vma=False)
```

time: 446 us -> 52.1 us (0.12)
  waiting for transfers between devices: 310 us -> 0 us
  blocking collectives: 69.2 us -> 0 us
  Pallas kernels: 0 us -> 45.5 us
  local copies, waits for them, and re-layouts: 21.8 us -> 3.2 us
  starting transfers between devices: 18.6 us -> 0 us
  between operations: 16.8 us -> 0.64 us
  other arithmetic: 9.3 us -> 2.5 us
    psum x1 -> x0, waiting for transfers between devices: 277 us -> none  [from_root(): return lax.psum(kept, axis)]
    psum x1 -> x0, blocking collectives: 69.2 us -> none  [local(): grad_total = lax.psum(jnp.sum(grad * grad), ('dp', 'pipe'))]
    pallas_call x0 -> x1, Pallas kernels: none -> 45.5 us  [local(): pl.pallas_call(kernel, out_shape=(jax.ShapeDtypeStruct((K, D), f32),) * 3...]
    all_to_all x3 -> x0, waiting for transfers between devices: 33 us -> none  [the longest x1 12.5 us: local(): lax.all_to_all(to_buffer(m_next), 'dp', split_axis=0, concat_axis=0, tile...]
    all_to_all x3 -> x0, starting transfers between devices: 18.6 us -> none  [the longest x1 9.98 us: local(): lax.all_to_all(to_buffer(w_next), 'dp', split_axis=0, concat_axis=0, tile...]
    gather x7 -> x0, local copies, waits for them, and re-layouts: 7.83 us -> none  [the longest x3 4.46 us: local(): values.reshape(ranks_count * peer_slots, row_width)[recv_index]]
    reshape x4 -> x0, local copies, waits for them, and re-layouts: 6.33 us -> none  [the longest x3 6.25 us: to_buffer(): return values[send_index].reshape(ranks_count, peer_slots, row_width)]
  transfers between devices with their start and end apart: 4 -> 0, of which waited for: 4 -> 0; matrix products, arithmetic and copies ran while one was open for 4% -> 0% of each run, Pallas kernels for 0% -> 0%
where the time goes in v1:
time: 52.1 us; the launch traced here: 51.9 us
  Pallas kernels  45.5 us (87%)
  local copies, waits for them, and re-layouts  3.2 us (6%)
  other arithmetic  2.5 us (5%)
  between operations  0.64 us (1%)
    pallas_call x1, Pallas kernels, local(): pl.pallas_call(kernel, out_shape=(jax.ShapeDtypeStruct((K, D), f32),) * 3...  45.5 us
    unnamed x2, local copies, waits for them, and re-layouts  3.2 us
    broadcast_in_dim x1, other arithmetic, local(): (corr_two * root * root)[None]  2.5 us

profile of v1, /device:TPU:0, one launch (start us, length us, event | category | flops | bytes accessed | tf_op | source)
XLA Modules:
  0.0 51.9 jit_solution(13161390932902923454)
XLA Ops:
  0.6 1.3 %copy.11.failed_ref = s32[4,2]{1,0:T(4,128)} copy(s32[4,2]{0,1:T(2,128)} %param.14) | data formatting | bytes 64 | tf_op args[6]
  2.0 45.5 %recover_step.1 = (f32[16,8192]{1,0:T(8,128)}, f32[16,8192]{1,0:T(8,128)}, f32[16,8192]{1,0:T(8,128)}) custom-call(f32[16,8192]{1,0:T(8,128)} %bitcast.12, f32[16,8192]{1,0:T(8,128)} %bitcast.13, f32[16,8192]{1,0:T(8,128)} %bitcast.14, bf16[16,8192]{1,0:T(8,128)(2,1)} %bitcast.15, s32[1,16]{1,0:T(1,128)} %expo_ref.1, bf16[32,16,8192]{2,1,0:T(8,128)(2,1)} %bitcast.10, ...), custom_call_target="tpu_custom_call" | custom-call | tf_op jit(solution)/shard_map/recover_step/pallas_call | solution.py:457
  47.5 2.5 %fusion = (f32[1,16,8192]{2,1,0:T(8,128)}, f32[1,16,8192]{2,1,0:T(8,128)}) fusion(f32[16,8192]{1,0:T(8,128)} %get-tuple-element.8, f32[16,8192]{1,0:T(8,128)} %get-tuple-element.6, f32[16,8192]{1,0:T(8,128)} %get-tuple-element.7), kind=kLoop, calls=%fused_computation.1 | loop fusion | flops 1179648 | bytes 2621440 | tf_op jit(solution)/shard_map/broadcast_in_dim | solution.py:511
  50.0 1.9 %copy.13 = f32[1,16,8192]{2,1,0:T(8,128)} copy(f32[1,16,8192]{2,1,0:T(8,128)} %bitcast.11) | data formatting | bytes 1048576

commit v2 on v1

v2 whole, which is shorter than its diff:
```python
import functools
import math

import jax
import jax.numpy as jnp
from jax import lax
from jax.experimental import pallas as pl
from jax.experimental.pallas import tpu as pltpu
from jax.sharding import PartitionSpec as P

STEP = 20

beta_one = 0.9
beta_two = 0.95
learn_rate = 0.00015
decay_rate = 0.1
adam_eps = 1e-08
clip_eps = 1e-06

corr_one = 1.0 - beta_one**STEP
corr_two = 1.0 - beta_two**STEP

LOGICAL = pl.DeviceIdType.LOGICAL
DP = 32
PIPE = 4
K = 16
D = 8192
HALF = D // 2
LANES = 128
W_COLS = HALF + 3 * LANES
PIECES = (2048, 2048, 2048, 1024, 1024)
BASES = tuple(sum(PIECES[:i]) for i in range(len(PIECES)))
WIDE = 1024
TILES = WIDE // LANES
STRIDE = 5
EARLY = 8

SCALE_UNIT = 65536.0
TINY = 1e-30
LOG_LOW = -2.2
LOG_SPAN = 16.0
LOG_UNIT = 65535.0 / LOG_SPAN


def cols(step, base=0):
    return pl.ds(pl.multiple_of(base + step * WIDE, LANES), WIDE)


def tiled(scale):
    return jnp.concatenate([scale] * TILES, axis=1)


def fold(acc, op):
    out = acc[:, :LANES]
    for t in range(1, TILES):
        out = op(out, acc[:, t * LANES : (t + 1) * LANES])
    return out


def scale_code(scale):
    return jnp.ceil(jnp.log2(jnp.maximum(scale, TINY)) * SCALE_UNIT).astype(jnp.int32)


def scale_value(code):
    return jnp.exp2(code.astype(jnp.float32) * (1.0 / SCALE_UNIT))


def nearest(x):
    return jnp.floor(x + 0.5).astype(jnp.int32)


def kernel(
    master_ref, moment1_ref, moment2_ref, quant_ref, expo_ref, replica_ref, failed_ref, dest_ref,
    w_ref, r_ref, u_ref,
    master, moment1, moment2, quant, expo, replica, dest_v, failed_s, dest_s,
    part, near, parts, w_code, w_send, w_recv, w_rows, mv_code, mv_send, mv_recvs, mv_rows,
    scales, lost_rows, amount, w_slot_s, mv_slot_s, owner_s, sender_s, local_s,
    in_sem, near_sem, part_sem, w_sem, mv_sem,
):
    me = lax.axis_index("dp")
    group = lax.axis_index("pipe")

    def member(rank, section):
        return rank * PIPE + section

    def rank_at(c):
        return lax.rem(me + c, DP)

    loads = [
        pltpu.make_async_copy(src, dst, in_sem.at[i])
        for i, (src, dst) in enumerate(
            (
                (quant_ref, quant),
                (expo_ref, expo),
                (dest_ref, dest_v),
                (dest_ref, dest_s),
                (failed_ref, failed_s),
                (master_ref, master),
                (moment1_ref, moment1),
                (replica_ref, replica),
                (moment2_ref, moment2),
            )
        )
    ]
    barrier = pltpu.get_barrier_semaphore()

    def greet(device):
        pl.semaphore_signal(barrier, inc=1, device_id=device, device_id_type=LOGICAL)

    for q in range(1, PIPE):
        greet(member(me, lax.rem(group + q, PIPE)))
    for c in range(1, DP):
        greet(member(rank_at(c), group))
    for load in loads:
        load.start()

    loads[0].wait()
    loads[1].wait()
    line = lax.broadcasted_iota(jnp.int32, (K, K), 0)
    place = lax.broadcasted_iota(jnp.int32, (K, K), 1)
    expo_rows = jnp.sum(
        jnp.where(line == place, jnp.broadcast_to(expo[...].astype(jnp.float32), (K, K)), 0.0),
        axis=1,
        keepdims=True,
    )
    grad_scale = jnp.exp2(expo_rows)

    def scan_grad(step, carry):
        total, largest = carry
        x = quant[:, cols(step)].astype(jnp.float32)
        return total + x * x, jnp.maximum(largest, jnp.abs(x))

    zero_step = jnp.zeros((K, WIDE), jnp.float32)
    total, largest = lax.fori_loop(0, D // WIDE, scan_grad, (zero_step, zero_step))
    squares = fold(total, jnp.add) * (grad_scale * grad_scale)
    part[0:1, :] = jnp.sum(squares, axis=0, keepdims=True)
    grad_code = scale_code(fold(largest, jnp.maximum) * ((1.0 - beta_one) * grad_scale))

    for load in loads[2:5]:
        load.wait()
    fail_a = failed_s[0, group]
    fail_b = failed_s[1, group]
    me_failed = (me == fail_a) | (me == fail_b)

    held = jnp.int32(0)
    words = [jnp.int32(0)] * 4
    for i in range(K):
        target = dest_s[group, me * K + i] >> 4
        nibble = i << (4 * (target & 7))
        words = [word | jnp.where((target >> 3) == q, nibble, 0) for q, word in enumerate(words)]
        held = held | (1 << target)

    dest_row = dest_v[pl.ds(group, 1), :]
    old_row = lax.broadcasted_iota(jnp.int32, (1, DP * K), 1)
    old_rank = old_row >> 4
    new_rank = dest_row >> 4
    alive_bits = ~((1 << fail_a) | (1 << fail_b))

    def helper_bits(receiver):
        bits = jnp.sum(jnp.where(new_rank == receiver, 1 << old_rank, 0))
        return alive_bits & ~bits

    def helper_row(receiver):
        bits = helper_bits(receiver)
        first = jnp.max(jnp.where((new_rank == receiver) & (old_rank == fail_a), old_row & 15, 0))
        second = jnp.max(jnp.where((new_rank == receiver) & (old_rank == fail_b), old_row & 15, 0))
        able = ((bits >> me) & 1) == 1
        lower = bits & ((1 << me) - 1)
        is_first = able & (lower == 0)
        is_second = able & (lower != 0) & ((lower & (lower - 1)) == 0)
        return jnp.where(is_first, K + first, jnp.where(is_second, 2 * K + second, 0))

    help_a = helper_row(fail_a)
    help_b = helper_row(fail_b)

    def fill_slot(c, carry):
        target = rank_at(c)
        word = words[0]
        for q in range(1, 4):
            word = jnp.where((target >> 3) == q, words[q], word)
        row = (word >> (4 * (target & 7))) & 15
        helped = jnp.where(target == fail_a, help_a, jnp.where(target == fail_b, help_b, 0))
        mv_slot_s[c] = row
        w_slot_s[c] = jnp.where(((held >> target) & 1) == 1, row, helped)
        return carry

    lax.fori_loop(0, DP, fill_slot, 0)

    for load in loads[5:8]:
        load.wait()

    def weights(kind, step, base=0):
        if kind == 0:
            return master[:, cols(step, base)]
        rank = fail_a if kind == 1 else fail_b
        return replica[rank, :, cols(step, base)].astype(jnp.float32)

    def scan_moment(step, largest):
        return jnp.maximum(largest, jnp.abs(moment1[:, cols(step)]))

    keep = jnp.where(me_failed, 0.0, 1.0).astype(jnp.float32)
    largest = lax.fori_loop(0, D // WIDE, scan_moment, zero_step)
    moment_code = scale_code(fold(largest, jnp.maximum) * (keep * beta_one))
    scales[0:K, :] = scale_value(moment_code)
    scales[K : 2 * K, :] = scale_value(grad_code)

    for kind in range(3):
        rows = pl.ds(kind * K, K)

        def scan_weights(step, largest, kind=kind):
            return jnp.maximum(largest, jnp.abs(weights(kind, step)))

        largest = lax.fori_loop(0, D // WIDE, scan_weights, zero_step)
        code = scale_code(fold(largest, jnp.maximum))
        to_code = tiled(32767.0 / scale_value(code))
        w_code[rows, HALF : HALF + LANES] = code
        w_code[rows, HALF + LANES : HALF + 2 * LANES] = moment_code
        w_code[rows, HALF + 2 * LANES : HALF + 3 * LANES] = grad_code

        def code_weights(step, carry, kind=kind, rows=rows, to_code=to_code):
            low = nearest(weights(kind, step) * to_code)
            high = nearest(weights(kind, step, HALF) * to_code)
            w_code[rows, cols(step)] = (high << 16) | (low & 0xFFFF)
            return carry

        lax.fori_loop(0, HALF // WIDE, code_weights, 0)

    pl.semaphore_wait(barrier, PIPE - 1 + DP - 1)

    def waiting(slots, width, sem):
        held_bytes = amount.at[pl.ds(0, slots), :, pl.ds(0, width)]
        return pltpu.make_async_copy(held_bytes, held_bytes, sem)

    def send(src, dst, sems, device):
        pltpu.make_async_remote_copy(
            src_ref=src,
            dst_ref=dst,
            send_sem=sems.at[0],
            recv_sem=sems.at[1],
            device_id=device,
            device_id_type=LOGICAL,
        ).start()

    for q in range(1, PIPE):
        send(
            part.at[pl.ds(0, 1)],
            near.at[pl.ds(q - 1, 1)],
            near_sem,
            member(me, lax.rem(group + q, PIPE)),
        )

    def slot_of(k):
        return lax.rem(k * STRIDE, DP)

    def fill_w(k):
        c = slot_of(k)
        w_send[pl.ds(c - 1, 1), :] = w_code[pl.ds(w_slot_s[c], 1), :]

    def send_w(k):
        c = slot_of(k)
        send(
            w_send.at[pl.ds(c - 1, 1)],
            w_recv.at[pl.ds(c - 1, 1)],
            w_sem,
            member(rank_at(c), group),
        )

    def step_w(k, carry):
        fill_w(k)
        send_w(k - 1)
        return carry

    fill_w(1)
    lax.fori_loop(2, EARLY + 2, step_w, 0)

    waiting(PIPE - 1, LANES, near_sem.at[1]).wait()
    own_part = part[0:1, :] + near[0:1, :] + near[1:2, :] + near[2:3, :]
    parts[DP - 1 : DP, :] = own_part
    for k in range(1, DP):
        c = (k * STRIDE) % DP
        send(
            parts.at[pl.ds(DP - 1, 1)],
            parts.at[pl.ds(c - 1, 1)],
            part_sem,
            member(rank_at(c), group),
        )
    lax.fori_loop(EARLY + 2, DP, step_w, 0)
    send_w(DP - 1)
    w_recv[DP - 1 : DP, :] = w_code[pl.ds(w_slot_s[0], 1), :]

    bits = helper_bits(me)
    lane = lax.broadcasted_iota(jnp.int32, (1, LANES), 1)
    able = (lane < DP) & (((bits >> (lane & 31)) & 1) == 1)
    helper_one = jnp.min(jnp.where(able, lane, DP - 1))
    helper_two = jnp.min(jnp.where(able & (lane > helper_one), lane, DP - 1))

    def slot_from(rank):
        return (me - rank + (DP - 1)) & (DP - 1)

    def find_row(j, carry):
        row = jnp.max(jnp.where(dest_row == me * K + j, old_row, 0))
        owner = row >> 4
        in_second = owner == fail_b
        lost = (owner == fail_a) | in_second
        helper = jnp.where(in_second, helper_two, helper_one)
        block = jnp.where(in_second, 2 * K, K)
        owner_s[j] = slot_from(owner)
        sender_s[j] = slot_from(jnp.where(lost & me_failed, helper, owner))
        local_s[j] = jnp.where(lost & jnp.logical_not(me_failed), block + (row & 15), 0)
        lost_rows[pl.ds(j, 1), :] = jnp.broadcast_to(jnp.where(lost, 1.0, 0.0), (1, LANES))
        return carry

    lax.fori_loop(0, K, find_row, 0)

    loads[8].wait()
    waiting(DP - 1, LANES, part_sem.at[1]).wait()
    grad_total = jnp.sum(jnp.sum(parts[...], axis=0, keepdims=True), axis=1, keepdims=True)
    clip = jnp.minimum(1.0, lax.rsqrt(grad_total / float(DP * PIPE * K * D) + clip_eps))

    bound = scales[0:K, :] + clip * scales[K : 2 * K, :]
    to_unit = tiled(1.0 / bound)
    clip_scale = grad_scale * clip

    def code_moments(step, carry):
        here = cols(step)
        clipped = quant[:, here].astype(jnp.float32) * clip_scale
        first = (keep * beta_one) * moment1[:, here] + (1.0 - beta_one) * clipped
        second = (keep * beta_two) * moment2[:, here] + (1.0 - beta_two) * clipped * clipped
        root = jnp.sqrt(jnp.abs(first) * to_unit) * 32767.0
        high = nearest(jnp.where(first < 0.0, -root, root))
        level = (jnp.log2(jnp.maximum(second, 0.2)) - LOG_LOW) * LOG_UNIT
        low = nearest(jnp.clip(level, 0.0, 65535.0))
        mv_code[:, here] = (high << 16) | low
        return carry

    for piece, (base, width) in enumerate(zip(BASES, PIECES)):
        lax.fori_loop(base // WIDE, (base + width) // WIDE, code_moments, 0)
        span = pl.ds(base, width)

        def fill_mv(k, span=span):
            c = slot_of(k)
            mv_send[pl.ds(c - 1, 1), span] = mv_code[pl.ds(mv_slot_s[c], 1), span]

        def send_mv(k, span=span, piece=piece):
            c = slot_of(k)
            send(
                mv_send.at[pl.ds(c - 1, 1), span],
                mv_recvs[piece].at[pl.ds(c - 1, 1)],
                mv_sem.at[piece],
                member(rank_at(c), group),
            )

        def step_mv(k, carry, fill=fill_mv, send_one=send_mv):
            fill(k)
            send_one(k - 1)
            return carry

        fill_mv(1)
        lax.fori_loop(2, DP, step_mv, 0)
        send_mv(DP - 1)
        mv_recvs[piece][DP - 1 : DP, :] = mv_code[pl.ds(mv_slot_s[0], 1), span]

    waiting(DP - 1, W_COLS, w_sem.at[1]).wait()

    def place_w(j, carry):
        local = local_s[j]
        from_peer = w_recv[pl.ds(sender_s[j], 1), 0 : HALF + LANES]
        from_here = w_code[pl.ds(local, 1), 0 : HALF + LANES]
        w_rows[pl.ds(j, 1), 0 : HALF + LANES] = jnp.where(local > 0, from_here, from_peer)
        w_rows[pl.ds(j, 1), HALF + LANES : W_COLS] = w_recv[
            pl.ds(owner_s[j], 1), HALF + LANES : W_COLS
        ]
        return carry

    lax.fori_loop(0, K, place_w, 0)
    w_unit = tiled(scale_value(w_rows[:, HALF : HALF + LANES]) * (1.0 / 32767.0))

    def decode_w(step, carry):
        word = w_rows[:, cols(step)]
        w_ref[:, cols(step)] = ((word << 16) >> 16).astype(jnp.float32) * w_unit
        w_ref[:, cols(step, HALF)] = (word >> 16).astype(jnp.float32) * w_unit
        return carry

    lax.fori_loop(0, HALF // WIDE, decode_w, 0)
    came_bound = scale_value(w_rows[:, HALF + LANES : HALF + 2 * LANES]) + clip * scale_value(
        w_rows[:, HALF + 2 * LANES : W_COLS]
    )
    from_unit = tiled(jnp.sqrt(came_bound) * (1.0 / 32767.0))
    row_lost = tiled(lost_rows[...]) > 0.5

    def decode_mv(step, carry):
        here = cols(step)
        word = mv_rows[:, here]
        signed_root = (word >> 16).astype(jnp.float32) * from_unit
        low = (word & 0xFFFF).astype(jnp.float32)
        grown = jnp.exp2(low * (0.5 / LOG_UNIT) + 0.5 * (LOG_LOW - math.log2(corr_two)))
        r_ref[:, here] = signed_root
        u_ref[:, here] = jnp.where(
            row_lost, signed_root * signed_root * math.sqrt(5.0 / corr_two), grown
        )
        return carry

    for piece, (base, width) in enumerate(zip(BASES, PIECES)):
        waiting(DP - 1, width, mv_sem.at[piece, 1]).wait()

        def place_mv(j, carry, piece=piece, base=base, width=width):
            mv_rows[pl.ds(j, 1), pl.ds(base, width)] = mv_recvs[piece][pl.ds(owner_s[j], 1), :]
            return carry

        lax.fori_loop(0, K, place_mv, 0)
        lax.fori_loop(base // WIDE, (base + width) // WIDE, decode_mv, 0)

    waiting(PIPE - 1, LANES, near_sem.at[0]).wait()
    waiting(DP - 1, LANES, part_sem.at[0]).wait()
    waiting(DP - 1, W_COLS, w_sem.at[0]).wait()
    for piece, width in enumerate(PIECES):
        waiting(DP - 1, width, mv_sem.at[piece, 0]).wait()


def local(master, moment1, moment2, quant_grad, grad_exponent, replica_params, failed, dest):
    f32, i32 = jnp.float32, jnp.int32
    hbm = pl.BlockSpec(memory_space=pltpu.HBM)
    vmem = pl.BlockSpec(memory_space=pltpu.VMEM)
    dma = pltpu.SemaphoreType.DMA
    start, signed_root, root = pl.pallas_call(
        kernel,
        out_shape=(jax.ShapeDtypeStruct((K, D), f32),) * 3,
        in_specs=[hbm] * 8,
        out_specs=(vmem,) * 3,
        scratch_shapes=[
            pltpu.VMEM((K, D), f32),
            pltpu.VMEM((K, D), f32),
            pltpu.VMEM((K, D), f32),
            pltpu.VMEM((K, D), jnp.bfloat16),
            pltpu.VMEM((1, K), i32),
            pltpu.VMEM((DP, K, D), jnp.bfloat16),
            pltpu.VMEM((PIPE, DP * K), i32),
            pltpu.SMEM((2, PIPE), i32),
            pltpu.SMEM((PIPE, DP * K), i32),
            pltpu.VMEM((8, LANES), f32),
            pltpu.VMEM((8, LANES), f32),
            pltpu.VMEM((DP, LANES), f32),
            pltpu.VMEM((3 * K, W_COLS), i32),
            pltpu.VMEM((DP, W_COLS), i32),
            pltpu.VMEM((DP, W_COLS), i32),
            pltpu.VMEM((K, W_COLS), i32),
            pltpu.VMEM((K, D), i32),
            pltpu.VMEM((DP, D), i32),
            [pltpu.VMEM((DP, width), i32) for width in PIECES],
            pltpu.VMEM((K, D), i32),
            pltpu.VMEM((2 * K, LANES), f32),
            pltpu.VMEM((K, LANES), f32),
            pltpu.VMEM((DP - 1, 1, W_COLS), i32),
            pltpu.SMEM((DP,), i32),
            pltpu.SMEM((DP,), i32),
            pltpu.SMEM((K,), i32),
            pltpu.SMEM((K,), i32),
            pltpu.SMEM((K,), i32),
            dma((9,)),
            dma((2,)),
            dma((2,)),
            dma((2,)),
            dma((len(PIECES), 2)),
        ],
        compiler_params=pltpu.CompilerParams(
            collective_id=0, has_side_effects=True, vmem_limit_bytes=24 * 2**20
        ),
        name="recover_step",
    )(
        *(
            pltpu.with_memory_space_constraint(x, pltpu.HBM)
            for x in (
                master[0],
                moment1[0],
                moment2[0],
                quant_grad[0],
                grad_exponent,
                replica_params[0, 0].reshape(DP, K, D),
                failed.T,
                dest,
            )
        )
    )
    first = signed_root * jnp.abs(signed_root)
    direction = first / corr_one / (root + adam_eps) + decay_rate * start
    return (
        (start - learn_rate * direction)[None],
        first[None],
        (corr_two * root * root)[None],
    )


def solution(mesh):
    in_specs = (
        P("pipe", "dp", None),
        P("pipe", "dp", None),
        P("pipe", "dp", None),
        P("pipe", "dp", None),
        P("pipe", "dp"),
        P("pipe", "dp", None, None),
        P(),
        P(),
    )
    out_specs = (P("pipe", "dp", None), P("pipe", "dp", None), P("pipe", "dp", None))
    return jax.shard_map(local, mesh=mesh, in_specs=in_specs, out_specs=out_specs, check_vma=False)
```

time: 52.1 us -> 36.7 us (0.70)
  Pallas kernels: 45.5 us -> 34.6 us
  local copies, waits for them, and re-layouts: 3.2 us -> 0 us
  other arithmetic: 2.5 us -> 1.33 us
    pallas_call x1, Pallas kernels: 45.5 us -> 34.6 us  [local(): pl.pallas_call(kernel, out_shape=(jax.ShapeDtypeStruct((K, D), f32),) * 3...]
    unnamed x2 -> x0, local copies, waits for them, and re-layouts: 3.2 us -> none
    broadcast_in_dim x1, other arithmetic: 2.5 us -> 1.33 us  [local(): (corr_two * root * root)[None]]
where the time goes in v2:
time: 36.7 us; the launch traced here: 36.6 us
  Pallas kernels  34.6 us (94%)
  other arithmetic  1.33 us (4%)
  between operations  0.64 us (2%)
    pallas_call x1, Pallas kernels, local(): pl.pallas_call(kernel, out_shape=(jax.ShapeDtypeStruct((K, D), f32),) * 3...  34.6 us
    broadcast_in_dim x1, other arithmetic, local(): (corr_two * root * root)[None]  1.33 us

profile of v2, /device:TPU:0, one launch (start us, length us, event | category | flops | bytes accessed | tf_op | source)
XLA Modules:
  0.0 36.6 jit_solution(12093815052284844022)
XLA Ops:
  0.6 34.6 %recover_step.1 = (f32[16,8192]{1,0:T(8,128)S(1)}, f32[16,8192]{1,0:T(8,128)S(1)}, f32[16,8192]{1,0:T(8,128)S(1)}) custom-call(f32[16,8192]{1,0:T(8,128)} %bitcast.13, f32[16,8192]{1,0:T(8,128)} %bitcast.14, f32[16,8192]{1,0:T(8,128)} %bitcast.15, bf16[16,8192]{1,0:T(8,128)(2,1)} %bitcast.16, s32[1,16]{1,0:T(1,128)} %expo_ref.1, ...), custom_call_target="tpu_custom_call" | custom-call | tf_op jit(solution)/shard_map/recover_step/pallas_call | solution.py:425
  35.3 1.3 %fusion = (f32[1,16,8192]{2,1,0:T(8,128)}, f32[1,16,8192]{2,1,0:T(8,128)}, f32[1,16,8192]{2,1,0:T(8,128)}) fusion(f32[16,8192]{1,0:T(8,128)S(1)} %get-tuple-element.8, f32[16,8192]{1,0:T(8,128)S(1)} %get-tuple-element.6, f32[16,8192]{1,0:T(8,128)S(1)} %get-tuple-element.7), kind=kLoop, calls=%fused_computation.2 | loop fusion | flops 1441792 | bytes 3145728 | tf_op jit(solution)/shard_map/broadcast_in_dim | solution.py:489

commit v3 on v2

--- a/solution.py
+++ b/solution.py
@@ -73,9 +73,9 @@
     master_ref, moment1_ref, moment2_ref, quant_ref, expo_ref, replica_ref, failed_ref, dest_ref,
     w_ref, r_ref, u_ref,
     master, moment1, moment2, quant, expo, replica, dest_v, failed_s, dest_s,
-    part, near, parts, w_code, w_send, w_recv, w_rows, mv_code, mv_send, mv_recvs, mv_rows,
+    part, near_parts, y_parts, x_parts, w_code, w_send, w_recv, w_rows, mv_code, mv_send, mv_recvs, mv_rows,
     scales, lost_rows, amount, w_slot_s, mv_slot_s, owner_s, sender_s, local_s,
-    in_sem, near_sem, part_sem, w_sem, mv_sem,
+    y_in, x_in, in_sem, near_sem, y_sem, x_sem, w_sem, mv_sem,
 ):
     me = lax.axis_index("dp")
     group = lax.axis_index("pipe")
@@ -107,10 +107,12 @@
     def greet(device):
         pl.semaphore_signal(barrier, inc=1, device_id=device, device_id_type=LOGICAL)
 
-    for q in range(1, PIPE):
-        greet(member(me, lax.rem(group + q, PIPE)))
-    for c in range(1, DP):
-        greet(member(rank_at(c), group))
+    flat = member(me, group)
+    column = [flat // 8 * 8 + lax.rem(flat + q, 8) for q in range(1, 8)]
+    along_y = [flat // 32 * 32 + lax.rem(flat + 8 * q, 32) for q in range(1, 4)]
+    along_x = [lax.rem(flat + 32 * q, 128) for q in range(1, 4)]
+    for device in (*column, *along_y, *along_x):
+        greet(device)
     for load in loads:
         load.start()
 
@@ -136,6 +138,26 @@
     part[0:1, :] = jnp.sum(squares, axis=0, keepdims=True)
     grad_code = scale_code(fold(largest, jnp.maximum) * ((1.0 - beta_one) * grad_scale))
 
+    def waiting(slots, width, sem):
+        held_bytes = amount.at[pl.ds(0, slots), :, pl.ds(0, width)]
+        return pltpu.make_async_copy(held_bytes, held_bytes, sem)
+
+    def send(src, dst, sems, device):
+        pltpu.make_async_remote_copy(
+            src_ref=src,
+            dst_ref=dst,
+            send_sem=sems.at[0],
+            recv_sem=sems.at[1],
+            device_id=device,
+            device_id_type=LOGICAL,
+        ).start()
+
+    pl.semaphore_wait(barrier, 13)
+    for q, device in enumerate(column):
+        send(part.at[pl.ds(0, 1)], near_parts.at[pl.ds(q, 1)], near_sem, device)
+    for device in along_y:
+        pl.semaphore_signal(y_in, inc=1, device_id=device, device_id_type=LOGICAL)
+
     for load in loads[2:5]:
         load.wait()
     fail_a = failed_s[0, group]
@@ -225,29 +247,16 @@
 
         lax.fori_loop(0, HALF // WIDE, code_weights, 0)
 
-    pl.semaphore_wait(barrier, PIPE - 1 + DP - 1)
-
-    def waiting(slots, width, sem):
-        held_bytes = amount.at[pl.ds(0, slots), :, pl.ds(0, width)]
-        return pltpu.make_async_copy(held_bytes, held_bytes, sem)
-
-    def send(src, dst, sems, device):
-        pltpu.make_async_remote_copy(
-            src_ref=src,
-            dst_ref=dst,
-            send_sem=sems.at[0],
-            recv_sem=sems.at[1],
-            device_id=device,
-            device_id_type=LOGICAL,
-        ).start()
-
-    for q in range(1, PIPE):
-        send(
-            part.at[pl.ds(0, 1)],
-            near.at[pl.ds(q - 1, 1)],
-            near_sem,
-            member(me, lax.rem(group + q, PIPE)),
-        )
+    pl.semaphore_wait(y_in, 3)
+    for device in along_x:
+        pl.semaphore_signal(x_in, inc=1, device_id=device, device_id_type=LOGICAL)
+
+    waiting(7, LANES, near_sem.at[1]).wait()
+    part[1:2, :] = part[0:1, :] + jnp.sum(near_parts[0:7, :], axis=0, keepdims=True)
+    for q, device in enumerate(along_y):
+        send(part.at[pl.ds(1, 1)], y_parts.at[pl.ds(q, 1)], y_sem, device)
+
+    pl.semaphore_wait(x_in, 3)
 
     def slot_of(k):
         return lax.rem(k * STRIDE, DP)
@@ -273,17 +282,10 @@
     fill_w(1)
     lax.fori_loop(2, EARLY + 2, step_w, 0)
 
-    waiting(PIPE - 1, LANES, near_sem.at[1]).wait()
-    own_part = part[0:1, :] + near[0:1, :] + near[1:2, :] + near[2:3, :]
-    parts[DP - 1 : DP, :] = own_part
-    for k in range(1, DP):
-        c = (k * STRIDE) % DP
-        send(
-            parts.at[pl.ds(DP - 1, 1)],
-            parts.at[pl.ds(c - 1, 1)],
-            part_sem,
-            member(rank_at(c), group),
-        )
+    waiting(3, LANES, y_sem.at[1]).wait()
+    part[2:3, :] = part[1:2, :] + jnp.sum(y_parts[0:3, :], axis=0, keepdims=True)
+    for q, device in enumerate(along_x):
+        send(part.at[pl.ds(2, 1)], x_parts.at[pl.ds(q, 1)], x_sem, device)
     lax.fori_loop(EARLY + 2, DP, step_w, 0)
     send_w(DP - 1)
     w_recv[DP - 1 : DP, :] = w_code[pl.ds(w_slot_s[0], 1), :]
@@ -313,8 +315,10 @@
     lax.fori_loop(0, K, find_row, 0)
 
     loads[8].wait()
-    waiting(DP - 1, LANES, part_sem.at[1]).wait()
-    grad_total = jnp.sum(jnp.sum(parts[...], axis=0, keepdims=True), axis=1, keepdims=True)
+    waiting(3, LANES, x_sem.at[1]).wait()
+    grad_total = jnp.sum(
+        part[2:3, :] + jnp.sum(x_parts[0:3, :], axis=0, keepdims=True), axis=1, keepdims=True
+    )
     clip = jnp.minimum(1.0, lax.rsqrt(grad_total / float(DP * PIPE * K * D) + clip_eps))
 
     bound = scales[0:K, :] + clip * scales[K : 2 * K, :]
@@ -410,8 +414,9 @@
         lax.fori_loop(0, K, place_mv, 0)
         lax.fori_loop(base // WIDE, (base + width) // WIDE, decode_mv, 0)
 
-    waiting(PIPE - 1, LANES, near_sem.at[0]).wait()
-    waiting(DP - 1, LANES, part_sem.at[0]).wait()
+    waiting(7, LANES, near_sem.at[0]).wait()
+    waiting(3, LANES, y_sem.at[0]).wait()
+    waiting(3, LANES, x_sem.at[0]).wait()
     waiting(DP - 1, W_COLS, w_sem.at[0]).wait()
     for piece, width in enumerate(PIECES):
         waiting(DP - 1, width, mv_sem.at[piece, 0]).wait()
@@ -439,7 +444,8 @@
             pltpu.SMEM((PIPE, DP * K), i32),
             pltpu.VMEM((8, LANES), f32),
             pltpu.VMEM((8, LANES), f32),
-            pltpu.VMEM((DP, LANES), f32),
+            pltpu.VMEM((8, LANES), f32),
+            pltpu.VMEM((8, LANES), f32),
             pltpu.VMEM((3 * K, W_COLS), i32),
             pltpu.VMEM((DP, W_COLS), i32),
             pltpu.VMEM((DP, W_COLS), i32),
@@ -456,7 +462,10 @@
             pltpu.SMEM((K,), i32),
             pltpu.SMEM((K,), i32),
             pltpu.SMEM((K,), i32),
+            pltpu.SemaphoreType.REGULAR,
+            pltpu.SemaphoreType.REGULAR,
             dma((9,)),
+            dma((2,)),
             dma((2,)),
             dma((2,)),
             dma((2,)),

time: 36.7 us -> 35.5 us (0.967)
  Pallas kernels: 34.6 us -> 33.4 us
    pallas_call x1, Pallas kernels: 34.6 us -> 33.4 us  [local(): pl.pallas_call(kernel, out_shape=(jax.ShapeDtypeStruct((K, D), f32),) * 3...]
where the time goes in v3:
time: 35.5 us; the launch traced here: 35.3 us
  Pallas kernels  33.4 us (94%)
  other arithmetic  1.33 us (4%)
  between operations  0.64 us (2%)
    pallas_call x1, Pallas kernels, local(): pl.pallas_call(kernel, out_shape=(jax.ShapeDtypeStruct((K, D), f32),) * 3...  33.4 us
    broadcast_in_dim x1, other arithmetic, local(): (corr_two * root * root)[None]  1.33 us

profile of v3, /device:TPU:0, one launch (start us, length us, event | category | flops | bytes accessed | tf_op | source)
XLA Modules:
  0.0 35.3 jit_solution(1407000598683636220)
XLA Ops:
  0.6 33.4 %recover_step.1 = (f32[16,8192]{1,0:T(8,128)S(1)}, f32[16,8192]{1,0:T(8,128)S(1)}, f32[16,8192]{1,0:T(8,128)S(1)}) custom-call(f32[16,8192]{1,0:T(8,128)} %bitcast.13, f32[16,8192]{1,0:T(8,128)} %bitcast.14, f32[16,8192]{1,0:T(8,128)} %bitcast.15, bf16[16,8192]{1,0:T(8,128)(2,1)} %bitcast.16, s32[1,16]{1,0:T(1,128)} %expo_ref.1, ...), custom_call_target="tpu_custom_call" | custom-call | tf_op jit(solution)/shard_map/recover_step/pallas_call | solution.py:430
  34.0 1.3 %fusion = (f32[1,16,8192]{2,1,0:T(8,128)}, f32[1,16,8192]{2,1,0:T(8,128)}, f32[1,16,8192]{2,1,0:T(8,128)}) fusion(f32[16,8192]{1,0:T(8,128)S(1)} %get-tuple-element.8, f32[16,8192]{1,0:T(8,128)S(1)} %get-tuple-element.6, f32[16,8192]{1,0:T(8,128)S(1)} %get-tuple-element.7), kind=kLoop, calls=%fused_computation.2 | loop fusion | flops 1441792 | bytes 3145728 | tf_op jit(solution)/shard_map/broadcast_in_dim | solution.py:498

commit v4 on v3

--- a/solution.py
+++ b/solution.py
@@ -33,7 +33,6 @@
 WIDE = 1024
 TILES = WIDE // LANES
 STRIDE = 5
-EARLY = 8
 
 SCALE_UNIT = 65536.0
 TINY = 1e-30
@@ -73,9 +72,9 @@
     master_ref, moment1_ref, moment2_ref, quant_ref, expo_ref, replica_ref, failed_ref, dest_ref,
     w_ref, r_ref, u_ref,
     master, moment1, moment2, quant, expo, replica, dest_v, failed_s, dest_s,
-    part, near_parts, y_parts, x_parts, w_code, w_send, w_recv, w_rows, mv_code, mv_send, mv_recvs, mv_rows,
+    part, near_parts, far_parts, w_code, w_send, w_recv, w_rows, mv_code, mv_send, mv_recvs, mv_rows,
     scales, lost_rows, amount, w_slot_s, mv_slot_s, owner_s, sender_s, local_s,
-    y_in, x_in, in_sem, near_sem, y_sem, x_sem, w_sem, mv_sem,
+    y_in, x_in, in_sem, near_sem, far_sem, w_sem, mv_sem,
 ):
     me = lax.axis_index("dp")
     group = lax.axis_index("pipe")
@@ -83,8 +82,19 @@
     def member(rank, section):
         return rank * PIPE + section
 
+    x0, y0, z0 = lax.div(me, 8), lax.rem(lax.div(me, 2), 4), lax.rem(me, 2)
+
     def rank_at(c):
-        return lax.rem(me + c, DP)
+        x = lax.rem(x0 + c // 8, 4)
+        y = lax.rem(y0 + (c // 2) % 4, 4)
+        return x * 8 + y * 2 + lax.rem(z0 + c % 2, 2)
+
+    x_parts = [lax.rem(x0 + d, 4) * (8 * PIPE) for d in range(4)]
+    y_parts = [lax.rem(y0 + d, 4) * (2 * PIPE) for d in range(4)]
+    z_parts = [lax.rem(z0 + d, 2) * PIPE + group for d in range(2)]
+
+    def device_at(c):
+        return x_parts[c // 8] + y_parts[(c // 2) % 4] + z_parts[c % 2]
 
     loads = [
         pltpu.make_async_copy(src, dst, in_sem.at[i])
@@ -113,7 +123,7 @@
     along_x = [lax.rem(flat + 32 * q, 128) for q in range(1, 4)]
     for device in (*column, *along_y, *along_x):
         greet(device)
-    for load in loads:
+    for load in loads[:7]:
         load.start()
 
     loads[0].wait()
@@ -155,7 +165,7 @@
     pl.semaphore_wait(barrier, 13)
     for q, device in enumerate(column):
         send(part.at[pl.ds(0, 1)], near_parts.at[pl.ds(q, 1)], near_sem, device)
-    for device in along_y:
+    for device in (*along_y, device_at(1)):
         pl.semaphore_signal(y_in, inc=1, device_id=device, device_id_type=LOGICAL)
 
     for load in loads[2:5]:
@@ -177,6 +187,97 @@
     old_rank = old_row >> 4
     new_rank = dest_row >> 4
     alive_bits = ~((1 << fail_a) | (1 << fail_b))
+
+    def fill_slot(c, carry):
+        target = rank_at(c)
+        word = words[0]
+        for q in range(1, 4):
+            word = jnp.where((target >> 3) == q, words[q], word)
+        w_slot_s[c] = (word >> (4 * (target & 7))) & 15
+        return carry
+
+    lax.fori_loop(0, DP, fill_slot, 0)
+
+    loads[5].wait()
+    loads[6].wait()
+    loads[7].start()
+    loads[8].start()
+
+    def scan_moment(step, largest):
+        return jnp.maximum(largest, jnp.abs(moment1[:, cols(step)]))
+
+    keep = jnp.where(me_failed, 0.0, 1.0).astype(jnp.float32)
+    largest = lax.fori_loop(0, D // WIDE, scan_moment, zero_step)
+    moment_code = scale_code(fold(largest, jnp.maximum) * (keep * beta_one))
+    scales[0:K, :] = scale_value(moment_code)
+    scales[K : 2 * K, :] = scale_value(grad_code)
+    w_code[:, HALF + LANES : HALF + 2 * LANES] = moment_code
+    w_code[:, HALF + 2 * LANES : HALF + 3 * LANES] = grad_code
+
+    def code_block(weights, store):
+        def scan_weights(step, largest):
+            return jnp.maximum(largest, jnp.abs(weights(step)))
+
+        largest = lax.fori_loop(0, D // WIDE, scan_weights, zero_step)
+        code = scale_code(fold(largest, jnp.maximum))
+        to_code = tiled(32767.0 / scale_value(code))
+        store(pl.ds(HALF, LANES), code)
+
+        def code_weights(step, carry):
+            low = nearest(weights(step) * to_code)
+            high = nearest(weights(step, HALF) * to_code)
+            store(cols(step), (high << 16) | (low & 0xFFFF))
+            return carry
+
+        lax.fori_loop(0, HALF // WIDE, code_weights, 0)
+
+    def store_own(span, value):
+        w_code[:, span] = value
+
+    code_block(lambda step, base=0: master[:, cols(step, base)], store_own)
+
+    def fill_w(c):
+        w_send[pl.ds(c - 1, 1), :] = w_code[pl.ds(w_slot_s[c], 1), :]
+
+    def send_w(c):
+        send(
+            w_send.at[pl.ds(c - 1, 1)],
+            w_recv.at[pl.ds(c - 1, 1)],
+            w_sem,
+            device_at(c),
+        )
+
+    for c in (1, 2, 8, 6, 24, 4, 16):
+        fill_w(c)
+    for c in (1, 2, 8, 6, 24, 4, 16):
+        send_w(c)
+
+    pl.semaphore_wait(y_in, 4)
+    for device in along_x:
+        pl.semaphore_signal(x_in, inc=1, device_id=device, device_id_type=LOGICAL)
+
+    waiting(7, LANES, near_sem.at[1]).wait()
+    part[1:2, :] = part[0:1, :] + jnp.sum(near_parts[0:7, :], axis=0, keepdims=True)
+    for k in range(1, 16):
+        q = (k * STRIDE) % 16
+        send(
+            part.at[pl.ds(1, 1)],
+            far_parts.at[pl.ds(q - 1, 1)],
+            far_sem,
+            device_at(2 * q),
+        )
+
+    def send_group(codes):
+        fill_w(codes[0])
+        for before, c in zip(codes, codes[1:]):
+            fill_w(c)
+            send_w(before)
+        send_w(codes[-1])
+
+    send_group([3, 18, 9, 12, 5, 26, 17, 10, 7, 20, 25, 28, 14, 22, 30])
+    pl.semaphore_wait(x_in, 3)
+    send_group([21, 11, 31, 13, 27, 23, 19, 15, 29])
+    w_recv[DP - 1 : DP, :] = w_code[pl.ds(w_slot_s[0], 1), :]
 
     def helper_bits(receiver):
         bits = jnp.sum(jnp.where(new_rank == receiver, 1 << old_rank, 0))
@@ -195,100 +296,16 @@
     help_a = helper_row(fail_a)
     help_b = helper_row(fail_b)
 
-    def fill_slot(c, carry):
+    help_a = helper_row(fail_a)
+    help_b = helper_row(fail_b)
+
+    def fill_help(c, carry):
         target = rank_at(c)
-        word = words[0]
-        for q in range(1, 4):
-            word = jnp.where((target >> 3) == q, words[q], word)
-        row = (word >> (4 * (target & 7))) & 15
         helped = jnp.where(target == fail_a, help_a, jnp.where(target == fail_b, help_b, 0))
-        mv_slot_s[c] = row
-        w_slot_s[c] = jnp.where(((held >> target) & 1) == 1, row, helped)
-        return carry
-
-    lax.fori_loop(0, DP, fill_slot, 0)
-
-    for load in loads[5:8]:
-        load.wait()
-
-    def weights(kind, step, base=0):
-        if kind == 0:
-            return master[:, cols(step, base)]
-        rank = fail_a if kind == 1 else fail_b
-        return replica[rank, :, cols(step, base)].astype(jnp.float32)
-
-    def scan_moment(step, largest):
-        return jnp.maximum(largest, jnp.abs(moment1[:, cols(step)]))
-
-    keep = jnp.where(me_failed, 0.0, 1.0).astype(jnp.float32)
-    largest = lax.fori_loop(0, D // WIDE, scan_moment, zero_step)
-    moment_code = scale_code(fold(largest, jnp.maximum) * (keep * beta_one))
-    scales[0:K, :] = scale_value(moment_code)
-    scales[K : 2 * K, :] = scale_value(grad_code)
-
-    for kind in range(3):
-        rows = pl.ds(kind * K, K)
-
-        def scan_weights(step, largest, kind=kind):
-            return jnp.maximum(largest, jnp.abs(weights(kind, step)))
-
-        largest = lax.fori_loop(0, D // WIDE, scan_weights, zero_step)
-        code = scale_code(fold(largest, jnp.maximum))
-        to_code = tiled(32767.0 / scale_value(code))
-        w_code[rows, HALF : HALF + LANES] = code
-        w_code[rows, HALF + LANES : HALF + 2 * LANES] = moment_code
-        w_code[rows, HALF + 2 * LANES : HALF + 3 * LANES] = grad_code
-
-        def code_weights(step, carry, kind=kind, rows=rows, to_code=to_code):
-            low = nearest(weights(kind, step) * to_code)
-            high = nearest(weights(kind, step, HALF) * to_code)
-            w_code[rows, cols(step)] = (high << 16) | (low & 0xFFFF)
-            return carry
-
-        lax.fori_loop(0, HALF // WIDE, code_weights, 0)
-
-    pl.semaphore_wait(y_in, 3)
-    for device in along_x:
-        pl.semaphore_signal(x_in, inc=1, device_id=device, device_id_type=LOGICAL)
-
-    waiting(7, LANES, near_sem.at[1]).wait()
-    part[1:2, :] = part[0:1, :] + jnp.sum(near_parts[0:7, :], axis=0, keepdims=True)
-    for q, device in enumerate(along_y):
-        send(part.at[pl.ds(1, 1)], y_parts.at[pl.ds(q, 1)], y_sem, device)
-
-    pl.semaphore_wait(x_in, 3)
-
-    def slot_of(k):
-        return lax.rem(k * STRIDE, DP)
-
-    def fill_w(k):
-        c = slot_of(k)
-        w_send[pl.ds(c - 1, 1), :] = w_code[pl.ds(w_slot_s[c], 1), :]
-
-    def send_w(k):
-        c = slot_of(k)
-        send(
-            w_send.at[pl.ds(c - 1, 1)],
-            w_recv.at[pl.ds(c - 1, 1)],
-            w_sem,
-            member(rank_at(c), group),
-        )
-
-    def step_w(k, carry):
-        fill_w(k)
-        send_w(k - 1)
-        return carry
-
-    fill_w(1)
-    lax.fori_loop(2, EARLY + 2, step_w, 0)
-
-    waiting(3, LANES, y_sem.at[1]).wait()
-    part[2:3, :] = part[1:2, :] + jnp.sum(y_parts[0:3, :], axis=0, keepdims=True)
-    for q, device in enumerate(along_x):
-        send(part.at[pl.ds(2, 1)], x_parts.at[pl.ds(q, 1)], x_sem, device)
-    lax.fori_loop(EARLY + 2, DP, step_w, 0)
-    send_w(DP - 1)
-    w_recv[DP - 1 : DP, :] = w_code[pl.ds(w_slot_s[0], 1), :]
+        mv_slot_s[c] = jnp.where(((held >> target) & 1) == 1, w_slot_s[c], helped)
+        return carry
+
+    lax.fori_loop(0, DP, fill_help, 0)
 
     bits = helper_bits(me)
     lane = lax.broadcasted_iota(jnp.int32, (1, LANES), 1)
@@ -297,7 +314,10 @@
     helper_two = jnp.min(jnp.where(able & (lane > helper_one), lane, DP - 1))
 
     def slot_from(rank):
-        return (me - rank + (DP - 1)) & (DP - 1)
+        x = (x0 - (rank >> 3)) & 3
+        y = (y0 - ((rank >> 1) & 3)) & 3
+        z = (z0 - (rank & 1)) & 1
+        return (x * 8 + y * 2 + z - 1) & (DP - 1)
 
     def find_row(j, carry):
         row = jnp.max(jnp.where(dest_row == me * K + j, old_row, 0))
@@ -307,17 +327,28 @@
         helper = jnp.where(in_second, helper_two, helper_one)
         block = jnp.where(in_second, 2 * K, K)
         owner_s[j] = slot_from(owner)
-        sender_s[j] = slot_from(jnp.where(lost & me_failed, helper, owner))
+        sender_s[j] = jnp.where(lost & me_failed, slot_from(helper), DP)
         local_s[j] = jnp.where(lost & jnp.logical_not(me_failed), block + (row & 15), 0)
         lost_rows[pl.ds(j, 1), :] = jnp.broadcast_to(jnp.where(lost, 1.0, 0.0), (1, LANES))
         return carry
 
     lax.fori_loop(0, K, find_row, 0)
 
+    loads[7].wait()
+    for kind, rank in ((1, fail_a), (2, fail_b)):
+
+        def store_lost(span, value, rows=pl.ds(kind * K, K)):
+            mv_code[rows, span] = value
+
+        code_block(
+            lambda step, base=0, rank=rank: replica[rank, :, cols(step, base)].astype(jnp.float32),
+            store_lost,
+        )
+
     loads[8].wait()
-    waiting(3, LANES, x_sem.at[1]).wait()
+    waiting(15, LANES, far_sem.at[1]).wait()
     grad_total = jnp.sum(
-        part[2:3, :] + jnp.sum(x_parts[0:3, :], axis=0, keepdims=True), axis=1, keepdims=True
+        part[1:2, :] + jnp.sum(far_parts[0:15, :], axis=0, keepdims=True), axis=1, keepdims=True
     )
     clip = jnp.minimum(1.0, lax.rsqrt(grad_total / float(DP * PIPE * K * D) + clip_eps))
 
@@ -334,63 +365,74 @@
         high = nearest(jnp.where(first < 0.0, -root, root))
         level = (jnp.log2(jnp.maximum(second, 0.2)) - LOG_LOW) * LOG_UNIT
         low = nearest(jnp.clip(level, 0.0, 65535.0))
-        mv_code[:, here] = (high << 16) | low
+        mv_code[0:K, here] = (high << 16) | low
         return carry
 
     for piece, (base, width) in enumerate(zip(BASES, PIECES)):
         lax.fori_loop(base // WIDE, (base + width) // WIDE, code_moments, 0)
         span = pl.ds(base, width)
 
-        def fill_mv(k, span=span):
-            c = slot_of(k)
+        def fill_mv(c, span=span):
             mv_send[pl.ds(c - 1, 1), span] = mv_code[pl.ds(mv_slot_s[c], 1), span]
 
-        def send_mv(k, span=span, piece=piece):
-            c = slot_of(k)
+        def send_mv(c, span=span, piece=piece):
             send(
                 mv_send.at[pl.ds(c - 1, 1), span],
                 mv_recvs[piece].at[pl.ds(c - 1, 1)],
                 mv_sem.at[piece],
-                member(rank_at(c), group),
+                device_at(c),
             )
 
-        def step_mv(k, carry, fill=fill_mv, send_one=send_mv):
-            fill(k)
-            send_one(k - 1)
-            return carry
-
-        fill_mv(1)
-        lax.fori_loop(2, DP, step_mv, 0)
-        send_mv(DP - 1)
+        codes = [k * STRIDE % DP for k in range(1, DP)]
+        fill_mv(codes[0])
+        for before, c in zip(codes, codes[1:]):
+            fill_mv(c)
+            send_mv(before)
+        send_mv(codes[-1])
         mv_recvs[piece][DP - 1 : DP, :] = mv_code[pl.ds(mv_slot_s[0], 1), span]
 
     waiting(DP - 1, W_COLS, w_sem.at[1]).wait()
 
-    def place_w(j, carry):
-        local = local_s[j]
-        from_peer = w_recv[pl.ds(sender_s[j], 1), 0 : HALF + LANES]
-        from_here = w_code[pl.ds(local, 1), 0 : HALF + LANES]
-        w_rows[pl.ds(j, 1), 0 : HALF + LANES] = jnp.where(local > 0, from_here, from_peer)
+    def place_scales(j, carry):
         w_rows[pl.ds(j, 1), HALF + LANES : W_COLS] = w_recv[
             pl.ds(owner_s[j], 1), HALF + LANES : W_COLS
         ]
         return carry
 
-    lax.fori_loop(0, K, place_w, 0)
-    w_unit = tiled(scale_value(w_rows[:, HALF : HALF + LANES]) * (1.0 / 32767.0))
-
-    def decode_w(step, carry):
-        word = w_rows[:, cols(step)]
-        w_ref[:, cols(step)] = ((word << 16) >> 16).astype(jnp.float32) * w_unit
-        w_ref[:, cols(step, HALF)] = (word >> 16).astype(jnp.float32) * w_unit
-        return carry
-
-    lax.fori_loop(0, HALF // WIDE, decode_w, 0)
+    lax.fori_loop(0, K, place_scales, 0)
     came_bound = scale_value(w_rows[:, HALF + LANES : HALF + 2 * LANES]) + clip * scale_value(
         w_rows[:, HALF + 2 * LANES : W_COLS]
     )
     from_unit = tiled(jnp.sqrt(came_bound) * (1.0 / 32767.0))
     row_lost = tiled(lost_rows[...]) > 0.5
+
+    def place_w(j, carry):
+        local = local_s[j]
+        sender = sender_s[j]
+        helped = sender < DP
+        sender = jnp.minimum(sender, DP - 1)
+        for piece in range(3):
+            base = BASES[piece]
+            width = min(PIECES[piece], HALF + LANES - base)
+            span = pl.ds(base, max(width, 2 * LANES))
+            from_peer = w_recv[pl.ds(owner_s[j], 1), span]
+            from_here = mv_code[pl.ds(local, 1), span]
+            from_helper = mv_recvs[piece][pl.ds(sender, 1), 0 : max(width, 2 * LANES)]
+            words = jnp.where(helped, from_helper, jnp.where(local > 0, from_here, from_peer))
+            w_rows[pl.ds(j, 1), span] = words
+        return carry
+
+    def take_w():
+        lax.fori_loop(0, K, place_w, 0)
+        w_unit = tiled(scale_value(w_rows[:, HALF : HALF + LANES]) * (1.0 / 32767.0))
+
+        def decode_w(step, carry):
+            word = w_rows[:, cols(step)]
+            w_ref[:, cols(step)] = ((word << 16) >> 16).astype(jnp.float32) * w_unit
+            w_ref[:, cols(step, HALF)] = (word >> 16).astype(jnp.float32) * w_unit
+            return carry
+
+        lax.fori_loop(0, HALF // WIDE, decode_w, 0)
 
     def decode_mv(step, carry):
         here = cols(step)
@@ -413,10 +455,11 @@
 
         lax.fori_loop(0, K, place_mv, 0)
         lax.fori_loop(base // WIDE, (base + width) // WIDE, decode_mv, 0)
+        if piece == 2:
+            take_w()
 
     waiting(7, LANES, near_sem.at[0]).wait()
-    waiting(3, LANES, y_sem.at[0]).wait()
-    waiting(3, LANES, x_sem.at[0]).wait()
+    waiting(15, LANES, far_sem.at[0]).wait()
     waiting(DP - 1, W_COLS, w_sem.at[0]).wait()
     for piece, width in enumerate(PIECES):
         waiting(DP - 1, width, mv_sem.at[piece, 0]).wait()
@@ -444,13 +487,12 @@
             pltpu.SMEM((PIPE, DP * K), i32),
             pltpu.VMEM((8, LANES), f32),
             pltpu.VMEM((8, LANES), f32),
-            pltpu.VMEM((8, LANES), f32),
-            pltpu.VMEM((8, LANES), f32),
-            pltpu.VMEM((3 * K, W_COLS), i32),
+            pltpu.VMEM((16, LANES), f32),
+            pltpu.VMEM((K, W_COLS), i32),
             pltpu.VMEM((DP, W_COLS), i32),
             pltpu.VMEM((DP, W_COLS), i32),
             pltpu.VMEM((K, W_COLS), i32),
-            pltpu.VMEM((K, D), i32),
+            pltpu.VMEM((3 * K, D), i32),
             pltpu.VMEM((DP, D), i32),
             [pltpu.VMEM((DP, width), i32) for width in PIECES],
             pltpu.VMEM((K, D), i32),
@@ -465,7 +507,6 @@
             pltpu.SemaphoreType.REGULAR,
             pltpu.SemaphoreType.REGULAR,
             dma((9,)),
-            dma((2,)),
             dma((2,)),
             dma((2,)),
             dma((2,)),

time: 35.5 us -> 34.8 us (0.980)
  Pallas kernels: 33.4 us -> 32.7 us
    pallas_call x1, Pallas kernels: 33.4 us -> 32.7 us  [local(): pl.pallas_call(kernel, out_shape=(jax.ShapeDtypeStruct((K, D), f32),) * 3...]
where the time goes in v4:
time: 34.8 us; the launch traced here: 34.6 us
  Pallas kernels  32.7 us (94%)
  other arithmetic  1.33 us (4%)
  between operations  0.64 us (2%)
    pallas_call x1, Pallas kernels, local(): pl.pallas_call(kernel, out_shape=(jax.ShapeDtypeStruct((K, D), f32),) * 3...  32.7 us
    broadcast_in_dim x1, other arithmetic, local(): (corr_two * root * root)[None]  1.33 us

profile of v4, /device:TPU:0, one launch (start us, length us, event | category | flops | bytes accessed | tf_op | source)
XLA Modules:
  0.0 34.6 jit_solution(11566146814576398798)
XLA Ops:
  0.6 32.7 %recover_step.1 = (f32[16,8192]{1,0:T(8,128)S(1)}, f32[16,8192]{1,0:T(8,128)S(1)}, f32[16,8192]{1,0:T(8,128)S(1)}) custom-call(f32[16,8192]{1,0:T(8,128)} %bitcast.13, f32[16,8192]{1,0:T(8,128)} %bitcast.14, f32[16,8192]{1,0:T(8,128)} %bitcast.15, bf16[16,8192]{1,0:T(8,128)(2,1)} %bitcast.16, s32[1,16]{1,0:T(1,128)} %expo_ref.1, ...), custom_call_target="tpu_custom_call" | custom-call | tf_op jit(solution)/shard_map/recover_step/pallas_call | solution.py:473
  33.3 1.3 %fusion = (f32[1,16,8192]{2,1,0:T(8,128)}, f32[1,16,8192]{2,1,0:T(8,128)}, f32[1,16,8192]{2,1,0:T(8,128)}) fusion(f32[16,8192]{1,0:T(8,128)S(1)} %get-tuple-element.8, f32[16,8192]{1,0:T(8,128)S(1)} %get-tuple-element.6, f32[16,8192]{1,0:T(8,128)S(1)} %get-tuple-element.7), kind=kLoop, calls=%fused_computation.2 | loop fusion | flops 1441792 | bytes 3145728 | tf_op jit(solution)/shard_map/broadcast_in_dim | solution.py:539

commit v5 on v4

--- a/solution.py
+++ b/solution.py
@@ -256,6 +256,15 @@
     for device in along_x:
         pl.semaphore_signal(x_in, inc=1, device_id=device, device_id_type=LOGICAL)
 
+    def send_group(codes):
+        fill_w(codes[0])
+        for before, c in zip(codes, codes[1:]):
+            fill_w(c)
+            send_w(before)
+        send_w(codes[-1])
+
+    send_group([3, 18, 9, 12, 5, 26, 17, 10, 7, 20, 25, 28, 14, 22, 30])
+
     waiting(7, LANES, near_sem.at[1]).wait()
     part[1:2, :] = part[0:1, :] + jnp.sum(near_parts[0:7, :], axis=0, keepdims=True)
     for k in range(1, 16):
@@ -267,14 +276,6 @@
             device_at(2 * q),
         )
 
-    def send_group(codes):
-        fill_w(codes[0])
-        for before, c in zip(codes, codes[1:]):
-            fill_w(c)
-            send_w(before)
-        send_w(codes[-1])
-
-    send_group([3, 18, 9, 12, 5, 26, 17, 10, 7, 20, 25, 28, 14, 22, 30])
     pl.semaphore_wait(x_in, 3)
     send_group([21, 11, 31, 13, 27, 23, 19, 15, 29])
     w_recv[DP - 1 : DP, :] = w_code[pl.ds(w_slot_s[0], 1), :]
@@ -383,7 +384,7 @@
                 device_at(c),
             )
 
-        codes = [k * STRIDE % DP for k in range(1, DP)]
+        codes = [k * 27 % DP for k in range(1, DP)]
         fill_mv(codes[0])
         for before, c in zip(codes, codes[1:]):
             fill_mv(c)

time: 34.8 us -> 34.5 us (level)
  no operation moved by 1% of the time
where the time goes in v5:
time: 34.5 us; the launch traced here: 34.3 us
  Pallas kernels  32.4 us (94%)
  other arithmetic  1.33 us (4%)
  between operations  0.64 us (2%)
    pallas_call x1, Pallas kernels, local(): pl.pallas_call(kernel, out_shape=(jax.ShapeDtypeStruct((K, D), f32),) * 3...  32.4 us
    broadcast_in_dim x1, other arithmetic, local(): (corr_two * root * root)[None]  1.33 us

profile of v5, /device:TPU:0, one launch (start us, length us, event | category | flops | bytes accessed | tf_op | source)
XLA Modules:
  0.0 34.3 jit_solution(13839280609524534592)
XLA Ops:
  0.6 32.4 %recover_step.1 = (f32[16,8192]{1,0:T(8,128)S(1)}, f32[16,8192]{1,0:T(8,128)S(1)}, f32[16,8192]{1,0:T(8,128)S(1)}) custom-call(f32[16,8192]{1,0:T(8,128)} %bitcast.13, f32[16,8192]{1,0:T(8,128)} %bitcast.14, f32[16,8192]{1,0:T(8,128)} %bitcast.15, bf16[16,8192]{1,0:T(8,128)(2,1)} %bitcast.16, s32[1,16]{1,0:T(1,128)} %expo_ref.1, ...), custom_call_target="tpu_custom_call" | custom-call | tf_op jit(solution)/shard_map/recover_step/pallas_call | solution.py:474
  33.0 1.3 %fusion = (f32[1,16,8192]{2,1,0:T(8,128)}, f32[1,16,8192]{2,1,0:T(8,128)}, f32[1,16,8192]{2,1,0:T(8,128)}) fusion(f32[16,8192]{1,0:T(8,128)S(1)} %get-tuple-element.8, f32[16,8192]{1,0:T(8,128)S(1)} %get-tuple-element.6, f32[16,8192]{1,0:T(8,128)S(1)} %get-tuple-element.7), kind=kLoop, calls=%fused_computation.2 | loop fusion | flops 1441792 | bytes 3145728 | tf_op jit(solution)/shard_map/broadcast_in_dim | solution.py:540

commit v6 on v5

--- a/solution.py
+++ b/solution.py
@@ -200,8 +200,6 @@
 
     loads[5].wait()
     loads[6].wait()
-    loads[7].start()
-    loads[8].start()
 
     def scan_moment(step, largest):
         return jnp.maximum(largest, jnp.abs(moment1[:, cols(step)]))
@@ -278,6 +276,8 @@
 
     pl.semaphore_wait(x_in, 3)
     send_group([21, 11, 31, 13, 27, 23, 19, 15, 29])
+    loads[8].start()
+    loads[7].start()
     w_recv[DP - 1 : DP, :] = w_code[pl.ds(w_slot_s[0], 1), :]
 
     def helper_bits(receiver):

time: 34.5 us -> 34.5 us (level)
  no operation moved by 1% of the time
where the time goes in v6:
time: 34.5 us; the launch traced here: 34.3 us
  Pallas kernels  32.4 us (94%)
  other arithmetic  1.33 us (4%)
  between operations  0.64 us (2%)
    pallas_call x1, Pallas kernels, local(): pl.pallas_call(kernel, out_shape=(jax.ShapeDtypeStruct((K, D), f32),) * 3...  32.4 us
    broadcast_in_dim x1, other arithmetic, local(): (corr_two * root * root)[None]  1.33 us

profile of v6, /device:TPU:0, one launch (start us, length us, event | category | flops | bytes accessed | tf_op | source)
XLA Modules:
  0.0 34.3 jit_solution(15467644514805310689)
XLA Ops:
  0.6 32.4 %recover_step.1 = (f32[16,8192]{1,0:T(8,128)S(1)}, f32[16,8192]{1,0:T(8,128)S(1)}, f32[16,8192]{1,0:T(8,128)S(1)}) custom-call(f32[16,8192]{1,0:T(8,128)} %bitcast.13, f32[16,8192]{1,0:T(8,128)} %bitcast.14, f32[16,8192]{1,0:T(8,128)} %bitcast.15, bf16[16,8192]{1,0:T(8,128)(2,1)} %bitcast.16, s32[1,16]{1,0:T(1,128)} %expo_ref.1, ...), custom_call_target="tpu_custom_call" | custom-call | tf_op jit(solution)/shard_map/recover_step/pallas_call | solution.py:474
  33.0 1.3 %fusion = (f32[1,16,8192]{2,1,0:T(8,128)}, f32[1,16,8192]{2,1,0:T(8,128)}, f32[1,16,8192]{2,1,0:T(8,128)}) fusion(f32[16,8192]{1,0:T(8,128)S(1)} %get-tuple-element.8, f32[16,8192]{1,0:T(8,128)S(1)} %get-tuple-element.6, f32[16,8192]{1,0:T(8,128)S(1)} %get-tuple-element.7), kind=kLoop, calls=%fused_computation.2 | loop fusion | flops 1441792 | bytes 3145728 | tf_op jit(solution)/shard_map/broadcast_in_dim | solution.py:540
